TPU v7x, 8 devices: a whole 2x2x1 slice. The times are simulated.
8 devices in a mesh: dp: 1 (over z), tp: 2 (over y), sp: 4 (over x, core).
Axes of the slice: x: 2, y: 2, z: 1, core: 2. Of those that a mesh axis runs over, the one named last changes fastest.
Arguments:
- features: bfloat16 [2, 576, 1024], P('dp', 'sp')
- tokens: int32 [2, 512], P('dp', 'sp')
- lengths: int32 [2], P('dp')
- proj_w: bfloat16 [1024, 2048], replicated
- proj_b: bfloat16 [2048], replicated
- embed: bfloat16 [256000, 2048], P('tp')
- ln_attn: bfloat16 [2, 2048], replicated
- w_query: bfloat16 [2, 2048, 2048], P(None, None, 'tp')
- w_key: bfloat16 [2, 2048, 256], replicated
- w_value: bfloat16 [2, 2048, 256], replicated
- w_out: bfloat16 [2, 2048, 2048], P(None, 'tp')
- ln_mlp: bfloat16 [2, 2048], replicated
- w_gate: bfloat16 [2, 2048, 16384], P(None, None, 'tp')
- w_up: bfloat16 [2, 2048, 16384], P(None, None, 'tp')
- w_down: bfloat16 [2, 16384, 2048], P(None, 'tp')
Outputs:
- output 1: bfloat16 [2, 576, 2048], P('dp', 'sp')
- output 2: bfloat16 [2, 512, 2048], P('dp', 'sp')
- output 3: bfloat16 [2, 2, 2, 576, 256], P(None, None, 'dp', 'sp')
- output 4: bfloat16 [2, 2, 2, 512, 256], P(None, None, 'dp', 'sp')
All inputs are finite; a program needn't handle non-finite values.
Results may differ from a plain program's by a relative error of at most 0.0128077.
Values are sent between devices in bfloat16 or wider.
A program may use at most 3 GiB of HBM per device.

v0:
```python
import math
import jax
import jax.numpy as jnp
from jax import lax
from jax.sharding import PartitionSpec as P

NORM_EPS = 1e-6
ROPE_THETA = 10000.0
NUM_LAYERS = 2


def rms_norm(hidden, norm_gain):
    hid_f32 = hidden.astype(jnp.float32)
    mean_sq = jnp.mean(hid_f32 * hid_f32, axis=-1, keepdims=True)
    return (hid_f32 * lax.rsqrt(mean_sq + NORM_EPS) * (1.0 + norm_gain.astype(jnp.float32))).astype(jnp.bfloat16)


def rotary(vectors, cos_table, sin_table):
    half_dim = vectors.shape[-1] // 2
    first_half = vectors[..., :half_dim]
    second_half = vectors[..., half_dim:]
    return jnp.concatenate([first_half * cos_table - second_half * sin_table, second_half * cos_table + first_half * sin_table], axis=-1)


def rope_tables(positions, head_dim):
    half_dim = head_dim // 2
    inv_freq = ROPE_THETA ** (-jnp.arange(half_dim, dtype=jnp.float32) * (2.0 / head_dim))
    angles = positions.astype(jnp.float32)[:, None] * inv_freq[None, :]
    return jnp.cos(angles), jnp.sin(angles)


def solution(mesh):
    sp_size = mesh.shape["sp"]
    in_specs = (P("dp", "sp", None), P("dp", "sp"), P("dp"), P(), P(), P("tp", None), P(), P(None, None, "tp"), P(), P(), P(None, "tp", None), P(), P(None, None, "tp"), P(None, None, "tp"), P(None, "tp", None))
    out_specs = (P("dp", "sp", None), P("dp", "sp", None), P(None, None, "dp", "sp", None), P(None, None, "dp", "sp", None))

    def device_fn(features, tokens, lengths, proj_w, proj_b, embed, ln_attn, w_query, w_key, w_value, w_out, ln_mlp, w_gate, w_up, w_down):
        num_req, img_loc, _ = features.shape
        txt_loc = tokens.shape[1]
        seq_loc = img_loc + txt_loc
        model_width = proj_w.shape[1]
        head_dim = w_key.shape[2]
        heads_loc = w_query.shape[2] // head_dim
        rows_loc = embed.shape[0]
        shard_idx = lax.axis_index("sp")
        tp_idx = lax.axis_index("tp")

        img_rows = (jnp.einsum("bpc,cd->bpd", features, proj_w, preferred_element_type=jnp.float32) + proj_b.astype(jnp.float32)).astype(jnp.bfloat16)
        local_ids = tokens - tp_idx * rows_loc
        owned_row = (local_ids >= 0) & (local_ids < rows_loc)
        picked = jnp.take(embed, jnp.clip(local_ids, 0, rows_loc - 1), axis=0)
        picked = jnp.where(owned_row[..., None], picked, jnp.zeros((), jnp.bfloat16))
        txt_rows = (lax.psum(picked, "tp").astype(jnp.float32) * math.sqrt(model_width)).astype(jnp.bfloat16)
        hidden = jnp.concatenate([img_rows, txt_rows], axis=1)

        positions = jnp.concatenate([shard_idx * img_loc + jnp.arange(img_loc), img_loc * sp_size + shard_idx * txt_loc + jnp.arange(txt_loc)])
        cos_table, sin_table = rope_tables(positions, head_dim)
        slot_idx = jnp.arange(seq_loc)[None, :]
        text_index = jnp.arange(sp_size)[:, None] * txt_loc + slot_idx - img_loc
        key_valid = ((slot_idx < img_loc)[None] | (text_index[None] < lengths[:, None, None])).reshape(num_req, sp_size * seq_loc)

        cache_parts = []
        for layer_idx in range(NUM_LAYERS):
            normed = rms_norm(hidden, ln_attn[layer_idx])
            queries = jnp.einsum("bsd,dn->bsn", normed, w_query[layer_idx], preferred_element_type=jnp.float32).reshape(num_req, seq_loc, heads_loc, head_dim)
            queries = rotary(queries, cos_table[:, None, :], sin_table[:, None, :]).astype(jnp.bfloat16)
            key_rows = rotary(jnp.einsum("bsd,dk->bsk", normed, w_key[layer_idx], preferred_element_type=jnp.float32), cos_table, sin_table).astype(jnp.bfloat16)
            value_rows = jnp.einsum("bsd,dk->bsk", normed, w_value[layer_idx], preferred_element_type=jnp.float32).astype(jnp.bfloat16)
            kv_all = lax.all_gather(jnp.concatenate([key_rows, value_rows], axis=-1), "sp", axis=1, tiled=True)
            scores = jnp.einsum("bqhk,bsk->bhqs", queries, kv_all[..., :head_dim], preferred_element_type=jnp.float32) * head_dim ** -0.5
            scores = jnp.where(key_valid[:, None, None, :], scores, -1e30)
            attn_probs = jax.nn.softmax(scores, axis=-1).astype(jnp.bfloat16)
            attn_heads = jnp.einsum("bhqs,bsk->bqhk", attn_probs, kv_all[..., head_dim:], preferred_element_type=jnp.float32).astype(jnp.bfloat16)
            attn_part = jnp.einsum("cril,ile->cre", attn_heads, w_out[layer_idx].reshape(heads_loc, head_dim, model_width), preferred_element_type=jnp.float32).astype(jnp.bfloat16)
            hidden = (hidden.astype(jnp.float32) + lax.psum(attn_part, "tp").astype(jnp.float32)).astype(jnp.bfloat16)
            normed = rms_norm(hidden, ln_mlp[layer_idx])
            gate_pre = jnp.einsum("bsd,df->bsf", normed, w_gate[layer_idx], preferred_element_type=jnp.float32)
            up_proj = jnp.einsum("bsd,df->bsf", normed, w_up[layer_idx], preferred_element_type=jnp.float32)
            mlp_mix = (jax.nn.gelu(gate_pre, approximate=True) * up_proj).astype(jnp.bfloat16)
            mlp_part = jnp.einsum("bsf,fd->bsd", mlp_mix, w_down[layer_idx], preferred_element_type=jnp.float32).astype(jnp.bfloat16)
            hidden = (hidden.astype(jnp.float32) + lax.psum(mlp_part, "tp").astype(jnp.float32)).astype(jnp.bfloat16)
            cache_parts.append(jnp.stack([key_rows, value_rows]))
        cache_loc = jnp.stack(cache_parts)
        return hidden[:, :img_loc], hidden[:, img_loc:], cache_loc[:, :, :, :img_loc], cache_loc[:, :, :, img_loc:]

    return jax.shard_map(device_fn, mesh=mesh, in_specs=in_specs, out_specs=out_specs, check_vma=False)
```

profile of v0, /device:TPU:0, one launch (start us, length us, event | category | flops | bytes accessed | tf_op | source)
XLA Modules:
  0.0 574.5 jit_solution(13888065074529820133)
XLA Ops:
  8.7 7.6 %gather_fusion = bf16[256,2048]{1,0:T(8,128)(2,1)S(1)} fusion(bf16[128000,2048]{1,0:T(8,128)(2,1)} %param.20, s32[1024]{0:T(1024)S(1)} %pad_clamp_fusion), kind=kCustom, calls=%fused_computation | custom fusion | bytes 2098176 | tf_op jit(solution)/shard_map/jit(_take)/gather | solution.py:51
  19.0 3.6 fusion.101
  22.6 32.4 %all-reduce.6.cloned.1.call-done = bf16[2,128,2048]{2,1,0:T(8,128)(2,1)} async-done(((bf16[2,128,2048]{2,1,0:T(8,128)(2,1)}), bf16[2,128,2048]{2,1,0:T(8,128)(2,1)}) %all-reduce.6.cloned.1.call-update) | async-done | bytes 1048592 | tf_op jit(solution)/shard_map/psum | solution.py:53
  57.0 2.2 convolution_convert_fusion.1
  61.9 6.0 %slice_bitcast_fusion = (bf16[1024,2048]{0,1:T(8,128)(2,1)}, bf16[1024,2048]{0,1:T(8,128)(2,1)}) fusion(bf16[2,2048,1024]{2,1,0:T(8,128)(2,1)} %param.22), kind=kLoop, calls=%fused_computation.101 | loop fusion | bytes 16777216 | tf_op jit(solution)/shard_map/bsd,dn->bsn/dot_general | solution.py:65
  67.9 6.5 %copy.19 = bf16[1024,2048]{1,0:T(8,128)(2,1)} copy(bf16[1024,2048]{0,1:T(8,128)(2,1)} %get-tuple-element.11) | data formatting | bytes 8388608 | tf_op jit(solution)/shard_map/bsd,dn->bsn/dot_general | solution.py:65
  74.5 6.5 %fusion.161 = (bf16[1,1024,2048]{2,1,0:T(8,128)(2,1)}, bf16[1,1024,2048]{2,1,0:T(8,128)(2,1)}) fusion(bf16[2,1024,2048]{2,1,0:T(8,128)(2,1)} %param.25), kind=kLoop, calls=%fused_computation.196 | loop fusion | bytes 16777216 | tf_op jit(solution)/shard_map/slice | solution.py:74
  81.0 2.6 fusion.106
  84.7 3.0 fusion.127
  87.8 5.5 fusion.162
  93.3 11.3 %bitcast_convert_fusion.1 = bf16[2,272,2048]{2,1,0:T(8,128)(2,1)} fusion(bf16[4,256,2048,1]{2,1,0,3:T(8,128)(2,1)} %bitcast.193, f32[2,4,272,1088]{3,2,1,0:T(8,128)} %get-tuple-element.31, f32[2,4,272]{2,1,0:T(4,128)S(1)} %get-tuple-element.30, bf16[2,1088,512]{2,1,0:T(8,128)(2,1)} %all-gather.3.cloned.1.call-done), kind=kOutput, calls=%fused_computation.98 | convolution fusion | flops 3500261376 | bytes 17572352 | tf_op jit(solution)/shard_map/cril,ile->cre/dot_general | solution.py:74
  105.5 59.3 %all-reduce.8.cloned.1.call-done = bf16[2,272,2048]{2,1,0:T(8,128)(2,1)} async-done(((bf16[2,272,2048]{2,1,0:T(8,128)(2,1)}), bf16[2,272,2048]{2,1,0:T(8,128)(2,1)}) %all-reduce.8.cloned.1.call-update) | async-done | bytes 2228240 | tf_op jit(solution)/shard_map/psum | solution.py:75
  164.7 3.8 fusion.74
  168.6 27.1 %fusion.12 = f32[2,272,8192]{2,1,0:T(8,128)} fusion(bf16[2,2048,8192]{2,1,0:T(8,128)(2,1)} %param.27, bf16[2,272,2048]{2,1,0:T(8,128)(2,1)} %get-tuple-element.9, f32[2048]{0:T(1024)S(1)} %bitcast.208, f32[2,272]{1,0:T(2,128)S(1)} %add_rsqrt_fusion.2), kind=kOutput, calls=%fused_computation.13 | convolution fusion | flops 18258067456 | bytes 53618816 | tf_op jit(solution)/shard_map/bsd,df->bsf/dot_general | solution.py:77
  195.7 28.2 %fusion.28.clone.7 = bf16[2,272,8192]{2,1,0:T(8,128)(2,1)} fusion(f32[2,272,8192]{2,1,0:T(8,128)} %fusion.12, bf16[2,2048,8192]{2,1,0:T(8,128)(2,1)} %param.28, bf16[2,272,2048]{2,1,0:T(8,128)(2,1)S(1)} %copy-done.3, f32[2048]{0:T(1024)S(1)} %bitcast.209, f32[2,272]{1,0:T(2,128)S(1)} %add_rsqrt_fusion.2), kind=kOutput, calls=%fused_computation.31.clone.clone.clone.clone.clone.2 | convolution fusion | flops 18302631936 | bytes 62531712 | tf_op jit(solution)/shard_map/bsd,df->bsf/dot_general | solution.py:78
  223.9 25.9 %fusion.88 = bf16[2,272,2048]{2,1,0:T(8,128)(2,1)} fusion(bf16[2,8192,2048]{2,1,0:T(8,128)(2,1)} %param.29, bf16[2,272,8192]{2,1,0:T(8,128)(2,1)} %fusion.28.clone.7), kind=kOutput, calls=%fused_computation.103 | convolution fusion | flops 18254725120 | bytes 44695552 | tf_op jit(solution)/shard_map/bsf,fd->bsd/dot_general | solution.py:80
  250.2 59.7 %all-reduce.10.cloned.1.call-done = bf16[2,272,2048]{2,1,0:T(8,128)(2,1)} async-done(((bf16[2,272,2048]{2,1,0:T(8,128)(2,1)}), bf16[2,272,2048]{2,1,0:T(8,128)(2,1)}) %all-reduce.10.cloned.1.call-update) | async-done | bytes 2228240 | tf_op jit(solution)/shard_map/psum | solution.py:81
  309.9 3.2 fusion.78
  313.1 2.2 convolution_convert_fusion
  317.4 6.5 %copy.20 = bf16[1024,2048]{1,0:T(8,128)(2,1)} copy(bf16[1024,2048]{0,1:T(8,128)(2,1)} %get-tuple-element.10) | data formatting | bytes 8388608 | tf_op jit(solution)/shard_map/bsd,dn->bsn/dot_general | solution.py:65
  323.9 4.7 fusion.104
  329.7 7.9 %all-gather.5.cloned.1.call-done = bf16[2,1088,512]{2,1,0:T(8,128)(2,1)} async-done(((bf16[2,272,512]{2,1,0:T(8,128)(2,1)}), bf16[2,1088,512]{2,1,0:T(8,128)(2,1)}) %all-gather.5.cloned.1.call-update) | async-done | bytes 2228240 | tf_op jit(solution)/shard_map/all_gather | solution.py:69
  337.7 3.0 fusion.126
  340.7 5.5 fusion.163
  346.2 11.3 %bitcast_convert_fusion = bf16[2,272,2048]{2,1,0:T(8,128)(2,1)} fusion(bf16[4,256,2048,1]{2,1,0,3:T(8,128)(2,1)} %bitcast.192, f32[2,4,272,1088]{3,2,1,0:T(8,128)} %get-tuple-element.33, f32[2,4,272]{2,1,0:T(4,128)S(1)} %get-tuple-element.32, bf16[2,1088,512]{2,1,0:T(8,128)(2,1)} %all-gather.5.cloned.1.call-done), kind=kOutput, calls=%fused_computation.97 | convolution fusion | flops 3500261376 | bytes 17572352 | tf_op jit(solution)/shard_map/cril,ile->cre/dot_general | solution.py:74
  357.7 59.9 %all-reduce.12.cloned.1.call-done = bf16[2,272,2048]{2,1,0:T(8,128)(2,1)} async-done(((bf16[2,272,2048]{2,1,0:T(8,128)(2,1)}), bf16[2,272,2048]{2,1,0:T(8,128)(2,1)}) %all-reduce.12.cloned.1.call-update) | async-done | bytes 2228240 | tf_op jit(solution)/shard_map/psum | solution.py:75
  417.6 3.8 fusion.82
  421.4 27.1 %fusion.6 = f32[2,272,8192]{2,1,0:T(8,128)} fusion(bf16[2,2048,8192]{2,1,0:T(8,128)(2,1)} %param.27, bf16[2,272,2048]{2,1,0:T(8,128)(2,1)} %get-tuple-element.5, f32[2048]{0:T(1024)S(1)} %bitcast.203, f32[2,272]{1,0:T(2,128)S(1)} %add_rsqrt_fusion), kind=kOutput, calls=%fused_computation.7 | convolution fusion | flops 18258067456 | bytes 53618816 | tf_op jit(solution)/shard_map/bsd,df->bsf/dot_general | solution.py:77
  448.5 28.2 %fusion.37.clone.7 = bf16[2,272,8192]{2,1,0:T(8,128)(2,1)} fusion(f32[2,272,8192]{2,1,0:T(8,128)} %fusion.6, bf16[2,2048,8192]{2,1,0:T(8,128)(2,1)} %param.28, bf16[2,272,2048]{2,1,0:T(8,128)(2,1)S(1)} %copy-done.2, f32[2048]{0:T(1024)S(1)} %bitcast.204, f32[2,272]{1,0:T(2,128)S(1)} %add_rsqrt_fusion), kind=kOutput, calls=%fused_computation.40.clone.clone.clone.clone.clone.2 | convolution fusion | flops 18302631936 | bytes 62531712 | tf_op jit(solution)/shard_map/bsd,df->bsf/dot_general | solution.py:78
  476.7 26.0 %fusion.93 = bf16[2,272,2048]{2,1,0:T(8,128)(2,1)} fusion(bf16[2,8192,2048]{2,1,0:T(8,128)(2,1)} %param.29, bf16[2,272,8192]{2,1,0:T(8,128)(2,1)} %fusion.37.clone.7), kind=kOutput, calls=%fused_computation.104 | convolution fusion | flops 18254725120 | bytes 44695552 | tf_op jit(solution)/shard_map/bsf,fd->bsd/dot_general | solution.py:80
  504.6 58.2 %all-reduce.14.cloned.1.call-done = bf16[2,272,2048]{2,1,0:T(8,128)(2,1)} async-done(((bf16[2,272,2048]{2,1,0:T(8,128)(2,1)}), bf16[2,272,2048]{2,1,0:T(8,128)(2,1)}) %all-reduce.14.cloned.1.call-update) | async-done | bytes 2228240 | tf_op jit(solution)/shard_map/psum | solution.py:81
  562.8 2.5 fusion.85
  (119 shorter events, 18.7 us)
Async XLA Ops:
  7.2 11.9 %copy-start = (bf16[2,144,1024]{2,1,0:T(8,128)(2,1)S(1)}, bf16[2,144,1024]{2,1,0:T(8,128)(2,1)}, u32[]{:S(2)}) copy-start(bf16[2,144,1024]{2,1,0:T(8,128)(2,1)} %param.15) | copy-start | bytes 1769476
  7.2 47.8 %all-reduce.6.cloned.1.call-start = ((), (), s32[]{:S(2)}) async-start(), calls=%async_computation | async-start | bytes 2097152 | tf_op jit(solution)/shard_map/psum | solution.py:53
  8.7 9.0 %copy-start.27 = (bf16[2048]{0:T(1024)(128)(2,1)S(1)}, bf16[2048]{0:T(1024)(128)(2,1)}, u32[]{:S(2)}) copy-start(bf16[2048]{0:T(1024)(128)(2,1)} %param.19) | copy-start | bytes 12292
  8.7 9.6 %copy-start.21 = (bf16[2,2048]{1,0:T(2,128)(2,1)S(1)}, bf16[2,2048]{1,0:T(2,128)(2,1)}, u32[]{:S(2)}) copy-start(bf16[2,2048]{1,0:T(2,128)(2,1)} %param.21) | copy-start | bytes 24580
  17.5 67.2 %all-gather.3.cloned.1.call-start = ((), (), s32[]{:S(2)}) async-start(), calls=%async_computation.1 | async-start | bytes 2785280 | tf_op jit(solution)/shard_map/all_gather | solution.py:69
  18.3 65.3 %copy-start.5 = (f32[272,128]{1,0:T(8,128)}, f32[272,128]{1,0:T(8,128)S(1)}, u32[]{:S(2)}) copy-start(f32[272,128]{1,0:T(8,128)S(1)} %get-tuple-element.26) | copy-start | bytes 417796
  18.3 65.3 %copy-start.7 = (f32[272,128]{1,0:T(8,128)}, f32[272,128]{1,0:T(8,128)S(1)}, u32[]{:S(2)}) copy-start(f32[272,128]{1,0:T(8,128)S(1)} %get-tuple-element.27) | copy-start | bytes 417796
  60.1 7.8 %copy-start.9 = (bf16[2,272,128]{2,1,0:T(8,128)(2,1)}, bf16[2,272,128]{2,1,0:T(8,128)(2,1)S(1)}, u32[]{:S(2)}) copy-start(bf16[2,272,128]{2,1,0:T(8,128)(2,1)S(1)} %get-tuple-element.20) | copy-start | bytes 417796
  60.1 7.8 %copy-start.11 = (bf16[2,272,128]{2,1,0:T(8,128)(2,1)}, bf16[2,272,128]{2,1,0:T(8,128)(2,1)S(1)}, u32[]{:S(2)}) copy-start(bf16[2,272,128]{2,1,0:T(8,128)(2,1)S(1)} %get-tuple-element.21) | copy-start | bytes 417796
  61.0 103.8 %all-reduce.8.cloned.1.call-start = ((), (), s32[]{:S(2)}) async-start(), calls=%async_computation.2 | async-start | bytes 4456448 | tf_op jit(solution)/shard_map/psum | solution.py:75
  67.9 6.5 %copy-start.28 = (s32[2]{0:T(128)S(1)}, s32[2]{0:T(128)}, u32[]{:S(2)}) copy-start(s32[2]{0:T(128)} %param.17) | copy-start | bytes 28
  74.5 13.3 %copy-start.25 = (pred[2,1088]{1,0:T(4,128)(4,1)}, pred[2,1088]{1,0:T(4,128)(4,1)S(1)}, u32[]{:S(2)}) copy-start(pred[2,1088]{1,0:T(4,128)(4,1)S(1)} %compare_or_fusion) | copy-start | bytes 6532
  74.5 6.5 %copy-start.4 = (bf16[1024,2048]{1,0:T(8,128)(2,1)S(1)}, bf16[1024,2048]{1,0:T(8,128)(2,1)}, u32[]{:S(2)}) copy-start(bf16[1024,2048]{1,0:T(8,128)(2,1)} %copy.19) | copy-start | bytes 12582916
  93.3 11.6 %copy-start.22 = (bf16[2,2048]{1,0:T(2,128)(2,1)S(1)}, bf16[2,2048]{1,0:T(2,128)(2,1)}, u32[]{:S(2)}) copy-start(bf16[2,2048]{1,0:T(2,128)(2,1)} %param.26) | copy-start | bytes 24580
  104.6 205.3 %all-reduce.10.cloned.1.call-start = ((), (), s32[]{:S(2)}) async-start(), calls=%async_computation.3 | async-start | bytes 4456448 | tf_op jit(solution)/shard_map/psum | solution.py:81
  168.6 27.1 %copy-start.3 = (bf16[2,272,2048]{2,1,0:T(8,128)(2,1)S(1)}, bf16[2,272,2048]{2,1,0:T(8,128)(2,1)}, u32[]{:S(2)}) copy-start(bf16[2,272,2048]{2,1,0:T(8,128)(2,1)} %get-tuple-element.9) | copy-start | bytes 6684676
  249.7 63.3 %copy-start.23 = (f32[1,2048]{1,0:T(1,128)S(1)}, f32[1,2048]{1,0:T(1,128)}, u32[]{:S(2)}) copy-start(f32[1,2048]{1,0:T(1,128)} %get-tuple-element.24) | copy-start | bytes 24580
  249.8 87.9 %all-gather.5.cloned.1.call-start = ((), (), s32[]{:S(2)}) async-start(), calls=%async_computation.4 | async-start | bytes 2785280 | tf_op jit(solution)/shard_map/all_gather | solution.py:69
  316.4 7.5 %copy-start.13 = (bf16[2,272,128]{2,1,0:T(8,128)(2,1)}, bf16[2,272,128]{2,1,0:T(8,128)(2,1)S(1)}, u32[]{:S(2)}) copy-start(bf16[2,272,128]{2,1,0:T(8,128)(2,1)S(1)} %get-tuple-element.18) | copy-start | bytes 417796
  316.5 7.5 %copy-start.15 = (bf16[2,272,128]{2,1,0:T(8,128)(2,1)}, bf16[2,272,128]{2,1,0:T(8,128)(2,1)S(1)}, u32[]{:S(2)}) copy-start(bf16[2,272,128]{2,1,0:T(8,128)(2,1)S(1)} %get-tuple-element.19) | copy-start | bytes 417796
  317.4 100.3 %all-reduce.12.cloned.1.call-start = ((), (), s32[]{:S(2)}) async-start(), calls=%async_computation.5 | async-start | bytes 4456448 | tf_op jit(solution)/shard_map/psum | solution.py:75
  337.7 3.1 copy-start.26
  357.5 63.9 %copy-start.24 = (f32[1,2048]{1,0:T(1,128)S(1)}, f32[1,2048]{1,0:T(1,128)}, u32[]{:S(2)}) copy-start(f32[1,2048]{1,0:T(1,128)} %get-tuple-element.22) | copy-start | bytes 24580
  357.5 205.3 %all-reduce.14.cloned.1.call-start = ((), (), s32[]{:S(2)}) async-start(), calls=%async_computation.6 | async-start | bytes 4456448 | tf_op jit(solution)/shard_map/psum | solution.py:81
  421.4 27.1 %copy-start.2 = (bf16[2,272,2048]{2,1,0:T(8,128)(2,1)S(1)}, bf16[2,272,2048]{2,1,0:T(8,128)(2,1)}, u32[]{:S(2)}) copy-start(bf16[2,272,2048]{2,1,0:T(8,128)(2,1)} %get-tuple-element.5) | copy-start | bytes 6684676
  476.7 26.0 %copy-start.10 = (bf16[2,272,128]{2,1,0:T(8,128)(2,1)S(1)}, bf16[2,272,128]{2,1,0:T(8,128)(2,1)}, u32[]{:S(2)}) copy-start(bf16[2,272,128]{2,1,0:T(8,128)(2,1)} %copy-done.9) | copy-start | bytes 417796
  476.7 26.0 %copy-start.12 = (bf16[2,272,128]{2,1,0:T(8,128)(2,1)S(1)}, bf16[2,272,128]{2,1,0:T(8,128)(2,1)}, u32[]{:S(2)}) copy-start(bf16[2,272,128]{2,1,0:T(8,128)(2,1)} %copy-done.11) | copy-start | bytes 417796
  476.7 26.1 %copy-start.18 = (bf16[2,272,256]{2,1,0:T(8,128)(2,1)S(1)}, bf16[2,272,256]{2,1,0:T(8,128)(2,1)}, u32[]{:S(2)}) copy-start(bf16[2,272,256]{2,1,0:T(8,128)(2,1)} %copy-done.17) | copy-start | bytes 835588
  476.7 26.1 %copy-start.14 = (bf16[2,272,128]{2,1,0:T(8,128)(2,1)S(1)}, bf16[2,272,128]{2,1,0:T(8,128)(2,1)}, u32[]{:S(2)}) copy-start(bf16[2,272,128]{2,1,0:T(8,128)(2,1)} %copy-done.13) | copy-start | bytes 417796
  476.7 26.1 %copy-start.16 = (bf16[2,272,128]{2,1,0:T(8,128)(2,1)S(1)}, bf16[2,272,128]{2,1,0:T(8,128)(2,1)}, u32[]{:S(2)}) copy-start(bf16[2,272,128]{2,1,0:T(8,128)(2,1)} %copy-done.15) | copy-start | bytes 417796
  476.7 26.1 %copy-start.20 = (bf16[2,272,256]{2,1,0:T(8,128)(2,1)S(1)}, bf16[2,272,256]{2,1,0:T(8,128)(2,1)}, u32[]{:S(2)}) copy-start(bf16[2,272,256]{2,1,0:T(8,128)(2,1)} %copy-done.19) | copy-start | bytes 835588
  503.7 63.8 %copy-start.1 = (bf16[2,144,1024]{2,1,0:T(8,128)(2,1)S(1)}, bf16[2,144,1024]{2,1,0:T(8,128)(2,1)}, u32[]{:S(2)}) copy-start(bf16[2,144,1024]{2,1,0:T(8,128)(2,1)} %param.15) | copy-start | bytes 1769476
  (6 other events, 8.6 us)
Sparse Core Ops, SparseCore 0:
  17.7 37.2 all-reduce.5
  61.1 20.1 all-gather.2
  104.7 59.9 all-reduce.7
  249.9 59.9 all-reduce.9
  317.5 20.1 all-gather.4
  357.6 59.9 all-reduce.11
  502.8 59.9 all-reduce.13
where the time goes:
time: 581 us; the launch traced here: 575 us
  waiting for transfers between devices  277 us (48%)
  matrix products  208 us (36%)
  other arithmetic  36.7 us (6%)
  local copies, waits for them, and re-layouts  36.1 us (6%)
  between operations  14.8 us (3%)
    psum x2, waiting for transfers between devices, device_fn(): lax.psum(attn_part, 'tp').astype(jnp.float32)  119 us
    psum x2, waiting for transfers between devices, device_fn(): lax.psum(mlp_part, 'tp').astype(jnp.float32)  118 us
    dot_general x2, matrix products, device_fn(): jnp.einsum('bsd,df->bsf', normed, w_up[layer_idx], preferred_element_type...  56.4 us
    dot_general x2, matrix products, device_fn(): jnp.einsum('bsd,df->bsf', normed, w_gate[layer_idx], preferred_element_ty...  54.2 us
    dot_general x2, matrix products, device_fn(): jnp.einsum('bsf,fd->bsd', mlp_mix, w_down[layer_idx], preferred_element_t...  51.8 us
    psum x1, waiting for transfers between devices, device_fn(): lax.psum(picked, 'tp').astype(jnp.float32) * math.sqrt(model_width)  32.4 us
    dot_general x2, matrix products, device_fn(): jnp.einsum('cril,ile->cre', attn_heads, w_out[layer_idx].reshape(heads_lo...  22.6 us
    dot_general x3, local copies, waits for them, and re-layouts, device_fn(): jnp.einsum('bsd,dn->bsn', normed, w_query[layer_idx], preferred_element_t...  19 us
  transfers between devices with their start and end apart: 7, of which 6 were waited for; matrix products, arithmetic and copies ran while one was open for 7% of the time, Pallas kernels for 0%

commit v1 on v0

v1 whole, which is shorter than its diff:
```python
import math
import jax
import jax.numpy as jnp
from jax import lax
from jax.sharding import PartitionSpec as P

NORM_EPS = 1e-6
ROPE_THETA = 10000.0
NUM_LAYERS = 2
SWAP = [(0, 1), (1, 0)]


def rms_norm(hidden, norm_gain):
    hid_f32 = hidden.astype(jnp.float32)
    mean_sq = jnp.mean(hid_f32 * hid_f32, axis=-1, keepdims=True)
    return (hid_f32 * lax.rsqrt(mean_sq + NORM_EPS) * (1.0 + norm_gain.astype(jnp.float32))).astype(jnp.bfloat16)


def rotary(vectors, cos_table, sin_table):
    half_dim = vectors.shape[-1] // 2
    first_half = vectors[..., :half_dim]
    second_half = vectors[..., half_dim:]
    return jnp.concatenate([first_half * cos_table - second_half * sin_table, second_half * cos_table + first_half * sin_table], axis=-1)


def rope_tables(positions, head_dim):
    half_dim = head_dim // 2
    inv_freq = ROPE_THETA ** (-jnp.arange(half_dim, dtype=jnp.float32) * (2.0 / head_dim))
    angles = positions.astype(jnp.float32)[:, None] * inv_freq[None, :]
    return jnp.cos(angles), jnp.sin(angles)


def dot32(a, b):
    return jnp.dot(a, b, preferred_element_type=jnp.float32)


def exchange_add(hidden, part):
    other = lax.ppermute(part, "tp", SWAP)
    total = (part.astype(jnp.float32) + other.astype(jnp.float32)).astype(jnp.bfloat16)
    return (hidden.astype(jnp.float32) + total.astype(jnp.float32)).astype(jnp.bfloat16)


def solution(mesh):
    sp_size = mesh.shape["sp"]
    in_specs = (P("dp", "sp", None), P("dp", "sp"), P("dp"), P(), P(), P("tp", None), P(), P(None, None, "tp"), P(), P(), P(None, "tp", None), P(), P(None, None, "tp"), P(None, None, "tp"), P(None, "tp", None))
    out_specs = (P("dp", "sp", None), P("dp", "sp", None), P(None, None, "dp", "sp", None), P(None, None, "dp", "sp", None))

    def device_fn(features, tokens, lengths, proj_w, proj_b, embed, ln_attn, w_query, w_key, w_value, w_out, ln_mlp, w_gate, w_up, w_down):
        num_req, img_loc, _ = features.shape
        txt_loc = tokens.shape[1]
        seq_loc = img_loc + txt_loc
        model_width = proj_w.shape[1]
        head_dim = w_key.shape[2]
        heads_loc = w_query.shape[2] // head_dim
        rows_loc = embed.shape[0]
        shard_idx = lax.axis_index("sp")
        tp_idx = lax.axis_index("tp")

        positions = jnp.concatenate([shard_idx * img_loc + jnp.arange(img_loc), img_loc * sp_size + shard_idx * txt_loc + jnp.arange(txt_loc)])
        cos_table, sin_table = rope_tables(positions, head_dim)
        slot_idx = jnp.arange(seq_loc)[None, :]
        text_index = jnp.arange(sp_size)[:, None] * txt_loc + slot_idx - img_loc

        hidden, key_valid = [], []
        for req in range(num_req):
            local_ids = tokens[req] - tp_idx * rows_loc
            owned_row = (local_ids >= 0) & (local_ids < rows_loc)
            picked = jnp.take(embed, jnp.clip(local_ids, 0, rows_loc - 1), axis=0)
            picked = jnp.where(owned_row[:, None], picked, jnp.zeros((), jnp.bfloat16))
            both = picked.astype(jnp.float32) + lax.ppermute(picked, "tp", SWAP).astype(jnp.float32)
            txt_rows = (both * math.sqrt(model_width)).astype(jnp.bfloat16)
            img_rows = (dot32(features[req], proj_w) + proj_b.astype(jnp.float32)).astype(jnp.bfloat16)
            hidden.append(jnp.concatenate([img_rows, txt_rows], axis=0))
            key_valid.append(((slot_idx < img_loc) | (text_index < lengths[req])).reshape(sp_size * seq_loc))

        cache_parts = []
        for layer_idx in range(NUM_LAYERS):
            kv_rows = []
            for req in range(num_req):
                normed = rms_norm(hidden[req], ln_attn[layer_idx])
                key_rows = rotary(dot32(normed, w_key[layer_idx]), cos_table, sin_table).astype(jnp.bfloat16)
                value_rows = dot32(normed, w_value[layer_idx]).astype(jnp.bfloat16)
                kv_rows.append(jnp.stack([key_rows, value_rows]))
                kv_all = lax.all_gather(jnp.concatenate([key_rows, value_rows], axis=-1), "sp", axis=0, tiled=True)
                queries = dot32(normed, w_query[layer_idx])
                heads = []
                for head in range(heads_loc):
                    query = rotary(queries[:, head * head_dim:(head + 1) * head_dim], cos_table, sin_table).astype(jnp.bfloat16)
                    scores = lax.dot_general(query, kv_all[:, :head_dim], (((1,), (1,)), ((), ())), preferred_element_type=jnp.float32) * head_dim ** -0.5
                    scores = jnp.where(key_valid[req][None, :], scores, -1e30)
                    probs = jax.nn.softmax(scores, axis=-1).astype(jnp.bfloat16)
                    heads.append(dot32(probs, kv_all[:, head_dim:]).astype(jnp.bfloat16))
                attn_part = dot32(jnp.concatenate(heads, axis=-1), w_out[layer_idx]).astype(jnp.bfloat16)
                hidden[req] = exchange_add(hidden[req], attn_part)
            for req in range(num_req):
                normed = rms_norm(hidden[req], ln_mlp[layer_idx])
                gate_pre = dot32(normed, w_gate[layer_idx])
                up_proj = dot32(normed, w_up[layer_idx])
                mlp_mix = (jax.nn.gelu(gate_pre, approximate=True) * up_proj).astype(jnp.bfloat16)
                hidden[req] = exchange_add(hidden[req], dot32(mlp_mix, w_down[layer_idx]).astype(jnp.bfloat16))
            cache_parts.append(jnp.stack(kv_rows, axis=1))
        cache_loc = jnp.stack(cache_parts)
        hidden = jnp.stack(hidden)
        return hidden[:, :img_loc], hidden[:, img_loc:], cache_loc[:, :, :, :img_loc], cache_loc[:, :, :, img_loc:]

    return jax.shard_map(device_fn, mesh=mesh, in_specs=in_specs, out_specs=out_specs, check_vma=False)
```

time: 581 us -> 463 us (0.80)
  waiting for transfers between devices: 277 us -> 94.2 us
  matrix products: 208 us -> 268 us
  starting transfers between devices: 1.51 us -> 14.7 us
  local copies, waits for them, and re-layouts: 36.1 us -> 25.6 us
    psum x5 -> x0, waiting for transfers between devices: 269 us -> none  [the longest x2 119 us: device_fn(): lax.psum(attn_part, 'tp').astype(jnp.float32)]
    ppermute x0 -> x10, waiting for transfers between devices: none -> 83.7 us  [the longest x8 74.8 us: exchange_add(): other = lax.ppermute(part, 'tp', SWAP)]
    dot_general x17 -> x62, matrix products: 208 us -> 268 us  [the longest x46 255 us: dot32(): return jnp.dot(a, b, preferred_element_type=jnp.float32)]
    dot_general x3 -> x0, local copies, waits for them, and re-layouts: 19 us -> none  [device_fn(): jnp.einsum('bsd,dn->bsn', normed, w_query[layer_idx], preferred_element_t...]
    unnamed x62 -> x126, local copies, waits for them, and re-layouts: 0.39 us -> 15.1 us
    ppermute x0 -> x10, starting transfers between devices: none -> 14.2 us  [the longest x8 10.9 us: exchange_add(): other = lax.ppermute(part, 'tp', SWAP)]
    sub x3 -> x0, other arithmetic: 11 us -> none  [the longest x2 11 us: device_fn(): attn_probs = jax.nn.softmax(scores, axis=-1).astype(jnp.bfloat16)]
    another operation x4 -> x15, other arithmetic: 2.38 us -> 12.7 us
  transfers between devices with their start and end apart: 7 -> 14, of which waited for: 6 -> 10; matrix products, arithmetic and copies ran while one was open for 7% -> 62% of each run, Pallas kernels for 0% -> 0%
where the time goes in v1:
time: 463 us; the launch traced here: 458 us
  matrix products  268 us (58%)
  waiting for transfers between devices  94.2 us (20%)
  other arithmetic  40.7 us (9%)
  local copies, waits for them, and re-layouts  25.6 us (6%)
  between operations  15 us (3%)
  starting transfers between devices  14.7 us (3%)
    dot_general x46, matrix products, dot32(): return jnp.dot(a, b, preferred_element_type=jnp.float32)  255 us
    ppermute x8, waiting for transfers between devices, exchange_add(): other = lax.ppermute(part, 'tp', SWAP)  74.8 us
    unnamed x126, local copies, waits for them, and re-layouts  15.1 us
    dot_general x16, matrix products, device_fn(): lax.dot_general(query, kv_all[:, :head_dim], (((1,), (1,)), ((), ())), pr...  12.6 us
    reduce_sum x8, other arithmetic, rms_norm(): mean_sq = jnp.mean(hid_f32 * hid_f32, axis=-1, keepdims=True)  12.3 us
    ppermute x8, starting transfers between devices, exchange_add(): other = lax.ppermute(part, 'tp', SWAP)  10.9 us
    all_gather x4, waiting for transfers between devices, device_fn(): lax.all_gather(jnp.concatenate([key_rows, value_rows], axis=-1), 'sp', ax...  10.4 us
  transfers between devices with their start and end apart: 14, of which 10 were waited for; matrix products, arithmetic and copies ran while one was open for 62% of the time, Pallas kernels for 0%

profile of v1, /device:TPU:0, one launch (start us, length us, event | category | flops | bytes accessed | tf_op | source)
XLA Modules:
  0.0 457.8 jit_solution(6677913939077632132)
XLA Ops:
  8.8 4.8 %gather_fusion.1 = bf16[128,2048]{1,0:T(8,128)(2,1)S(1)} fusion(bf16[128000,2048]{1,0:T(8,128)(2,1)} %param.22, s32[1024]{0:T(1024)S(1)} %pad_clamp_fusion), kind=kCustom, calls=%fused_computation.1.clone | custom fusion | bytes 1049088 | tf_op jit(solution)/shard_map/jit(_take)/gather | solution.py:68
  13.8 2.7 collective-permute-start.5
  16.6 3.0 fusion.185
  19.7 8.9 %collective-permute-done.5 = bf16[128,2048]{1,0:T(8,128)(2,1)S(1)} collective-permute-done((bf16[128,2048]{1,0:T(8,128)(2,1)S(1)}, bf16[128,2048]{1,0:T(8,128)(2,1)S(1)}, u32[]{:S(2)}, u32[]{:S(2)}) %collective-permute-start.5) | collective-permute-done | bytes 524320 | tf_op jit(solution)/shard_map/ppermute | solution.py:70
  33.1 4.3 gather_fusion
  39.5 3.6 fusion.124
  43.8 4.7 %all-gather.9.cloned.1.call-done = bf16[1088,512]{1,0:T(8,128)(2,1)} async-done(((bf16[272,512]{1,0:T(8,128)(2,1)}), bf16[1088,512]{1,0:T(8,128)(2,1)}) %all-gather.9.cloned.1.call-update) | async-done | bytes 1114128 | tf_op jit(solution)/shard_map/all_gather | solution.py:84
  62.1 3.1 fusion.184
  65.8 20.1 %collective-permute-done.6 = bf16[272,2048]{1,0:T(8,128)(2,1)} collective-permute-done((bf16[272,2048]{1,0:T(8,128)(2,1)S(1)}, bf16[272,2048]{1,0:T(8,128)(2,1)}, u32[]{:S(2)}, u32[]{:S(2)}) %collective-permute-start.6) | collective-permute-done | bytes 1114144 | tf_op jit(solution)/shard_map/ppermute | solution.py:38
  88.1 17.7 %fusion.20 = f32[272,8192]{1,0:T(8,128)} fusion(bf16[2,2048,8192]{2,1,0:T(8,128)(2,1)} %param.29, bf16[272,2048]{1,0:T(8,128)(2,1)S(1)} %get-tuple-element.14, f32[272]{0:T(512)S(1)} %add_rsqrt_fusion.2, f32[2048]{0:T(1024)S(1)} %bitcast.224), kind=kOutput, calls=%fused_computation.22 | convolution fusion | flops 9129033728 | bytes 43590720 | tf_op jit(solution)/shard_map/dot_general | solution.py:34
  105.9 18.8 %fusion.54.clone.7 = bf16[272,8192]{1,0:T(8,128)(2,1)} fusion(bf16[2,2048,8192]{2,1,0:T(8,128)(2,1)} %param.30, f32[272,8192]{1,0:T(8,128)} %fusion.20, bf16[272,2048]{1,0:T(8,128)(2,1)S(1)} %get-tuple-element.14, f32[272]{0:T(512)S(1)} %add_rsqrt_fusion.2, f32[2048]{0:T(1024)S(1)} %bitcast.225), kind=kOutput, calls=%fused_computation.48.clone.clone.clone.clone.clone.2 | convolution fusion | flops 9151315968 | bytes 48047168 | tf_op jit(solution)/shard_map/dot_general | solution.py:34
  124.7 17.8 %fusion.169 = bf16[272,2048]{1,0:T(8,128)(2,1)} fusion(bf16[2,8192,2048]{2,1,0:T(8,128)(2,1)} %param.31, bf16[272,8192]{1,0:T(8,128)(2,1)} %fusion.54.clone.7), kind=kOutput, calls=%fused_computation.179 | convolution fusion | flops 9127362560 | bytes 39124992 | tf_op jit(solution)/shard_map/dot_general | solution.py:34
  147.9 19.8 %collective-permute-done.7 = bf16[272,2048]{1,0:T(8,128)(2,1)S(1)} collective-permute-done((bf16[272,2048]{1,0:T(8,128)(2,1)}, bf16[272,2048]{1,0:T(8,128)(2,1)S(1)}, u32[]{:S(2)}, u32[]{:S(2)}) %collective-permute-start.7) | collective-permute-done | bytes 1114144 | tf_op jit(solution)/shard_map/ppermute | solution.py:38
  170.5 3.6 fusion.126
  177.7 3.5 fusion.116
  196.1 4.8 %all-gather.11.cloned.1.call-done = bf16[1088,512]{1,0:T(8,128)(2,1)} async-done(((bf16[272,512]{1,0:T(8,128)(2,1)}), bf16[1088,512]{1,0:T(8,128)(2,1)}) %all-gather.11.cloned.1.call-update) | async-done | bytes 1114128 | tf_op jit(solution)/shard_map/all_gather | solution.py:84
  208.9 2.4 fusion.161
  212.7 9.3 %collective-permute-done.1 = bf16[272,2048]{1,0:T(8,128)(2,1)} collective-permute-done((bf16[272,2048]{1,0:T(8,128)(2,1)S(1)}, bf16[272,2048]{1,0:T(8,128)(2,1)}, u32[]{:S(2)}, u32[]{:S(2)}) %collective-permute-start.1) | collective-permute-done | bytes 1114144 | tf_op jit(solution)/shard_map/ppermute | solution.py:38
  224.1 17.8 %fusion.22 = f32[272,8192]{1,0:T(8,128)} fusion(bf16[2,2048,8192]{2,1,0:T(8,128)(2,1)} %param.29, bf16[272,2048]{1,0:T(8,128)(2,1)S(1)} %get-tuple-element.22, f32[2048]{0:T(1024)S(1)} %bitcast.226, f32[272]{0:T(512)S(1)} %add_rsqrt_fusion.6), kind=kOutput, calls=%fused_computation.24 | convolution fusion | flops 9129033728 | bytes 43590720 | tf_op jit(solution)/shard_map/dot_general | solution.py:34
  241.8 18.8 %fusion.57.clone.7 = bf16[272,8192]{1,0:T(8,128)(2,1)} fusion(bf16[2,2048,8192]{2,1,0:T(8,128)(2,1)} %param.30, f32[272,8192]{1,0:T(8,128)} %fusion.22, bf16[272,2048]{1,0:T(8,128)(2,1)S(1)} %get-tuple-element.22, f32[2048]{0:T(1024)S(1)} %bitcast.227, f32[272]{0:T(512)S(1)} %add_rsqrt_fusion.6), kind=kOutput, calls=%fused_computation.49.clone.clone.clone.clone.clone.2 | convolution fusion | flops 9151315968 | bytes 48047168 | tf_op jit(solution)/shard_map/dot_general | solution.py:34
  260.7 17.4 %fusion.164 = bf16[272,2048]{1,0:T(8,128)(2,1)} fusion(bf16[2,8192,2048]{2,1,0:T(8,128)(2,1)} %param.31, bf16[272,8192]{1,0:T(8,128)(2,1)} %fusion.57.clone.7), kind=kOutput, calls=%fused_computation.178 | convolution fusion | flops 9127362560 | bytes 39124992 | tf_op jit(solution)/shard_map/dot_general | solution.py:34
  279.5 2.3 fusion.214
  281.8 17.9 %fusion.8 = f32[272,8192]{1,0:T(8,128)} fusion(bf16[2,2048,8192]{2,1,0:T(8,128)(2,1)} %param.29, bf16[272,2048]{1,0:T(8,128)(2,1)S(1)} %get-tuple-element.10, f32[272]{0:T(512)S(1)} %add_rsqrt_fusion, f32[2048]{0:T(1024)S(1)} %bitcast.220), kind=kOutput, calls=%fused_computation.10 | convolution fusion | flops 9129033728 | bytes 43590720 | tf_op jit(solution)/shard_map/dot_general | solution.py:34
  299.8 3.5 collective-permute-done.2
  309.8 19.3 %fusion.48.clone.7 = bf16[272,8192]{1,0:T(8,128)(2,1)} fusion(bf16[2,2048,8192]{2,1,0:T(8,128)(2,1)} %param.30, f32[272,8192]{1,0:T(8,128)} %fusion.8, bf16[272,2048]{1,0:T(8,128)(2,1)S(1)} %get-tuple-element.10, f32[272]{0:T(512)S(1)} %add_rsqrt_fusion, f32[2048]{0:T(1024)S(1)} %bitcast.221), kind=kOutput, calls=%fused_computation.46.clone.clone.clone.clone.clone.2 | convolution fusion | flops 9151315968 | bytes 48047168 | tf_op jit(solution)/shard_map/dot_general | solution.py:34
  329.2 3.6 fusion.118
  345.0 17.4 %fusion.179 = bf16[272,2048]{1,0:T(8,128)(2,1)} fusion(bf16[2,8192,2048]{2,1,0:T(8,128)(2,1)} %param.31, bf16[272,8192]{1,0:T(8,128)(2,1)} %fusion.48.clone.7), kind=kOutput, calls=%fused_computation.181 | convolution fusion | flops 9127362560 | bytes 39124992 | tf_op jit(solution)/shard_map/dot_general | solution.py:34
  362.9 8.0 %collective-permute-done.3 = bf16[272,2048]{1,0:T(8,128)(2,1)} collective-permute-done((bf16[272,2048]{1,0:T(8,128)(2,1)S(1)}, bf16[272,2048]{1,0:T(8,128)(2,1)}, u32[]{:S(2)}, u32[]{:S(2)}) %collective-permute-start.3) | collective-permute-done | bytes 1114144 | tf_op jit(solution)/shard_map/ppermute | solution.py:38
  373.2 17.8 %fusion.10 = f32[272,8192]{1,0:T(8,128)} fusion(bf16[2,2048,8192]{2,1,0:T(8,128)(2,1)} %param.29, bf16[272,2048]{1,0:T(8,128)(2,1)S(1)} %get-tuple-element.18, f32[2048]{0:T(1024)S(1)} %bitcast.222, f32[272]{0:T(512)S(1)} %add_rsqrt_fusion.4), kind=kOutput, calls=%fused_computation.12 | convolution fusion | flops 9129033728 | bytes 43590720 | tf_op jit(solution)/shard_map/dot_general | solution.py:34
  391.0 19.2 %fusion.51.clone.7 = bf16[272,8192]{1,0:T(8,128)(2,1)} fusion(bf16[2,2048,8192]{2,1,0:T(8,128)(2,1)} %param.30, f32[272,8192]{1,0:T(8,128)} %fusion.10, bf16[272,2048]{1,0:T(8,128)(2,1)S(1)} %get-tuple-element.18, f32[2048]{0:T(1024)S(1)} %bitcast.223, f32[272]{0:T(512)S(1)} %add_rsqrt_fusion.4), kind=kOutput, calls=%fused_computation.47.clone.clone.clone.clone.clone.2 | convolution fusion | flops 9151315968 | bytes 48047168 | tf_op jit(solution)/shard_map/dot_general | solution.py:34
  410.2 17.4 %fusion.174 = bf16[272,2048]{1,0:T(8,128)(2,1)} fusion(bf16[2,8192,2048]{2,1,0:T(8,128)(2,1)} %param.31, bf16[272,8192]{1,0:T(8,128)(2,1)} %fusion.51.clone.7), kind=kOutput, calls=%fused_computation.180 | convolution fusion | flops 9127362560 | bytes 39124992 | tf_op jit(solution)/shard_map/dot_general | solution.py:34
  434.2 14.1 %collective-permute-done.4 = bf16[272,2048]{1,0:T(8,128)(2,1)S(1)} collective-permute-done((bf16[272,2048]{1,0:T(8,128)(2,1)}, bf16[272,2048]{1,0:T(8,128)(2,1)S(1)}, u32[]{:S(2)}, u32[]{:S(2)}) %collective-permute-start.4) | collective-permute-done | bytes 1114144 | tf_op jit(solution)/shard_map/ppermute | solution.py:38
  (269 shorter events, 95.4 us)
Async XLA Ops:
  7.2 41.3 %all-gather.9.cloned.1.call-start = ((), (), s32[]{:S(2)}) async-start(), calls=%async_computation.2 | async-start | bytes 1392640 | tf_op jit(solution)/shard_map/all_gather | solution.py:84
  8.8 7.8 %copy-start.37 = (bf16[2048]{0:T(1024)(128)(2,1)S(1)}, bf16[2048]{0:T(1024)(128)(2,1)}, u32[]{:S(2)}) copy-start(bf16[2048]{0:T(1024)(128)(2,1)} %param.21) | copy-start | bytes 12292
  13.8 14.8 %collective-permute-start.5 = (bf16[128,2048]{1,0:T(8,128)(2,1)S(1)}, bf16[128,2048]{1,0:T(8,128)(2,1)S(1)}, u32[]{:S(2)}, u32[]{:S(2)}) collective-permute-start(bf16[128,2048]{1,0:T(8,128)(2,1)S(1)} %select_select_fusion), channel_id=1, source_target_pairs={{0,4},{4,0},{1,5},{5,1},{2,6},{6,2},{3,7},{7,3}} | collective-permute-start | bytes 1572872 | tf_op jit(solution)/shard_map/ppermute | solution.py:70
  19.6 155.2 %copy-start.29 = (f32[128]{0:T(128)}, f32[128]{0:T(128)S(1)}, u32[]{:S(2)}) copy-start(f32[128]{0:T(128)S(1)} %multiply_power_fusion) | copy-start | bytes 1540
  19.7 158.0 %copy-start.32 = (f32[1,2048]{1,0:T(1,128)}, f32[1,2048]{1,0:T(1,128)S(1)}, u32[]{:S(2)}) copy-start(f32[1,2048]{1,0:T(1,128)S(1)} %get-tuple-element.67) | copy-start | bytes 24580
  19.7 9.7 %copy-start.43 = (bf16[2,2048,256]{2,1,0:T(8,128)(2,1)S(1)}, bf16[2,2048,256]{2,1,0:T(8,128)(2,1)}, u32[]{:S(2)}) copy-start(bf16[2,2048,256]{2,1,0:T(8,128)(2,1)} %param.26) | copy-start | bytes 6291460
  32.8 151.8 %all-gather.5.cloned.1.call-start = ((), (), s32[]{:S(2)}) async-start(), calls=%async_computation | async-start | bytes 1392640 | tf_op jit(solution)/shard_map/all_gather | solution.py:84
  39.5 12.7 %copy-start.40 = (pred[1088]{0:T(1024)(128)(4,1)}, pred[1088]{0:T(1024)(128)(4,1)S(1)}, u32[]{:S(2)}) copy-start(pred[1088]{0:T(1024)(128)(4,1)S(1)} %or.34) | copy-start | bytes 3268
  58.4 27.5 %collective-permute-start.6 = (bf16[272,2048]{1,0:T(8,128)(2,1)S(1)}, bf16[272,2048]{1,0:T(8,128)(2,1)}, u32[]{:S(2)}, u32[]{:S(2)}) collective-permute-start(bf16[272,2048]{1,0:T(8,128)(2,1)S(1)} %fusion.155), channel_id=1, source_target_pairs={{0,4},{4,0},{1,5},{5,1},{2,6},{6,2},{3,7},{7,3}} | collective-permute-start | bytes 3342344 | tf_op jit(solution)/shard_map/ppermute | solution.py:38
  60.8 83.2 %collective-permute-start = (bf16[128,2048]{1,0:T(8,128)(2,1)}, bf16[128,2048]{1,0:T(8,128)(2,1)}, u32[]{:S(2)}, u32[]{:S(2)}) collective-permute-start(bf16[128,2048]{1,0:T(8,128)(2,1)} %select_select_fusion.1), channel_id=1, source_target_pairs={{0,4},{4,0},{1,5},{5,1},{2,6},{6,2},{3,7},{7,3}} | collective-permute-start | bytes 1572872 | tf_op jit(solution)/shard_map/ppermute | solution.py:70
  65.8 40.1 %copy-start.35 = (f32[1,2048]{1,0:T(1,128)}, f32[1,2048]{1,0:T(1,128)S(1)}, u32[]{:S(2)}) copy-start(f32[1,2048]{1,0:T(1,128)S(1)} %get-tuple-element.66) | copy-start | bytes 24580
  142.5 25.2 %collective-permute-start.7 = (bf16[272,2048]{1,0:T(8,128)(2,1)}, bf16[272,2048]{1,0:T(8,128)(2,1)S(1)}, u32[]{:S(2)}, u32[]{:S(2)}) collective-permute-start(bf16[272,2048]{1,0:T(8,128)(2,1)} %fusion.169), channel_id=1, source_target_pairs={{0,4},{4,0},{1,5},{5,1},{2,6},{6,2},{3,7},{7,3}} | collective-permute-start | bytes 3342344 | tf_op jit(solution)/shard_map/ppermute | solution.py:38
  147.4 20.4 %copy-start.6 = (bf16[272,2048]{1,0:T(8,128)(2,1)S(1)}, bf16[272,2048]{1,0:T(8,128)(2,1)}, u32[]{:S(2)}) copy-start(bf16[272,2048]{1,0:T(8,128)(2,1)} %fusion.169) | copy-start | bytes 3342340
  147.9 21.7 %copy-start.22 = (bf16[272,256]{1,0:T(8,128)(2,1)}, bf16[272,256]{1,0:T(8,128)(2,1)S(1)}, u32[]{:S(2)}) copy-start(bf16[272,256]{1,0:T(8,128)(2,1)S(1)} %convolution_convert_fusion.19) | copy-start | bytes 417796
  170.4 30.4 %all-gather.11.cloned.1.call-start = ((), (), s32[]{:S(2)}) async-start(), calls=%async_computation.3 | async-start | bytes 1392640 | tf_op jit(solution)/shard_map/all_gather | solution.py:84
  182.7 150.8 %all-gather.7.cloned.1.call-start = ((), (), s32[]{:S(2)}) async-start(), calls=%async_computation.1 | async-start | bytes 1392640 | tf_op jit(solution)/shard_map/all_gather | solution.py:84
  194.6 8.3 %copy-start.2 = (bf16[272,2048]{1,0:T(8,128)(2,1)}, bf16[272,2048]{1,0:T(8,128)(2,1)S(1)}, u32[]{:S(2)}) copy-start(bf16[272,2048]{1,0:T(8,128)(2,1)S(1)} %fusion.152) | copy-start | bytes 3342340
  194.6 27.5 %collective-permute-start.1 = (bf16[272,2048]{1,0:T(8,128)(2,1)S(1)}, bf16[272,2048]{1,0:T(8,128)(2,1)}, u32[]{:S(2)}, u32[]{:S(2)}) collective-permute-start(bf16[272,2048]{1,0:T(8,128)(2,1)S(1)} %fusion.152), channel_id=1, source_target_pairs={{0,4},{4,0},{1,5},{5,1},{2,6},{6,2},{3,7},{7,3}} | collective-permute-start | bytes 3342344 | tf_op jit(solution)/shard_map/ppermute | solution.py:38
  208.9 13.2 %copy-start.3 = (bf16[272,2048]{1,0:T(8,128)(2,1)S(1)}, bf16[272,2048]{1,0:T(8,128)(2,1)}, u32[]{:S(2)}) copy-start(bf16[272,2048]{1,0:T(8,128)(2,1)} %copy-done.2) | copy-start | bytes 3342340
  211.3 12.8 %copy-start.36 = (f32[1,2048]{1,0:T(1,128)S(1)}, f32[1,2048]{1,0:T(1,128)}, u32[]{:S(2)}) copy-start(f32[1,2048]{1,0:T(1,128)} %copy-done.35) | copy-start | bytes 24580
  211.3 68.3 %collective-permute-start.8 = (bf16[272,2048]{1,0:T(8,128)(2,1)}, bf16[272,2048]{1,0:T(8,128)(2,1)}, u32[]{:S(2)}, u32[]{:S(2)}) collective-permute-start(bf16[272,2048]{1,0:T(8,128)(2,1)} %fusion.161), channel_id=1, source_target_pairs={{0,4},{4,0},{1,5},{5,1},{2,6},{6,2},{3,7},{7,3}} | collective-permute-start | bytes 3342344 | tf_op jit(solution)/shard_map/ppermute | solution.py:38
  278.0 25.2 %collective-permute-start.2 = (bf16[272,2048]{1,0:T(8,128)(2,1)}, bf16[272,2048]{1,0:T(8,128)(2,1)}, u32[]{:S(2)}, u32[]{:S(2)}) collective-permute-start(bf16[272,2048]{1,0:T(8,128)(2,1)} %fusion.164), channel_id=1, source_target_pairs={{0,4},{4,0},{1,5},{5,1},{2,6},{6,2},{3,7},{7,3}} | collective-permute-start | bytes 3342344 | tf_op jit(solution)/shard_map/ppermute | solution.py:38
  343.5 18.9 %copy-start.7 = (bf16[272,2048]{1,0:T(8,128)(2,1)}, bf16[272,2048]{1,0:T(8,128)(2,1)S(1)}, u32[]{:S(2)}) copy-start(bf16[272,2048]{1,0:T(8,128)(2,1)S(1)} %fusion.158) | copy-start | bytes 3342340
  343.5 27.5 %collective-permute-start.3 = (bf16[272,2048]{1,0:T(8,128)(2,1)S(1)}, bf16[272,2048]{1,0:T(8,128)(2,1)}, u32[]{:S(2)}, u32[]{:S(2)}) collective-permute-start(bf16[272,2048]{1,0:T(8,128)(2,1)S(1)} %fusion.158), channel_id=1, source_target_pairs={{0,4},{4,0},{1,5},{5,1},{2,6},{6,2},{3,7},{7,3}} | collective-permute-start | bytes 3342344 | tf_op jit(solution)/shard_map/ppermute | solution.py:38
  362.4 69.6 %collective-permute-start.9 = (bf16[272,2048]{1,0:T(8,128)(2,1)}, bf16[272,2048]{1,0:T(8,128)(2,1)}, u32[]{:S(2)}, u32[]{:S(2)}) collective-permute-start(bf16[272,2048]{1,0:T(8,128)(2,1)} %fusion.179), channel_id=1, source_target_pairs={{0,4},{4,0},{1,5},{5,1},{2,6},{6,2},{3,7},{7,3}} | collective-permute-start | bytes 3342344 | tf_op jit(solution)/shard_map/ppermute | solution.py:38
  410.1 18.9 %copy-start.9 = (bf16[272,128]{1,0:T(8,128)(2,1)S(1)}, bf16[272,128]{1,0:T(8,128)(2,1)}, u32[]{:S(2)}) copy-start(bf16[272,128]{1,0:T(8,128)(2,1)} %copy-done.8) | copy-start | bytes 208900
  410.1 18.9 %copy-start.11 = (bf16[272,128]{1,0:T(8,128)(2,1)S(1)}, bf16[272,128]{1,0:T(8,128)(2,1)}, u32[]{:S(2)}) copy-start(bf16[272,128]{1,0:T(8,128)(2,1)} %copy-done.10) | copy-start | bytes 208900
  410.2 18.9 %copy-start.18 = (bf16[272,256]{1,0:T(8,128)(2,1)S(1)}, bf16[272,256]{1,0:T(8,128)(2,1)}, u32[]{:S(2)}) copy-start(bf16[272,256]{1,0:T(8,128)(2,1)} %copy-done.17) | copy-start | bytes 417796
  410.2 19.0 %copy-start.13 = (bf16[272,128]{1,0:T(8,128)(2,1)S(1)}, bf16[272,128]{1,0:T(8,128)(2,1)}, u32[]{:S(2)}) copy-start(bf16[272,128]{1,0:T(8,128)(2,1)} %copy-done.12) | copy-start | bytes 208900
  410.2 19.0 %copy-start.15 = (bf16[272,128]{1,0:T(8,128)(2,1)S(1)}, bf16[272,128]{1,0:T(8,128)(2,1)}, u32[]{:S(2)}) copy-start(bf16[272,128]{1,0:T(8,128)(2,1)} %copy-done.14) | copy-start | bytes 208900
  427.6 20.7 %collective-permute-start.4 = (bf16[272,2048]{1,0:T(8,128)(2,1)}, bf16[272,2048]{1,0:T(8,128)(2,1)S(1)}, u32[]{:S(2)}, u32[]{:S(2)}) collective-permute-start(bf16[272,2048]{1,0:T(8,128)(2,1)} %fusion.174), channel_id=1, source_target_pairs={{0,4},{4,0},{1,5},{5,1},{2,6},{6,2},{3,7},{7,3}} | collective-permute-start | bytes 3342344 | tf_op jit(solution)/shard_map/ppermute | solution.py:38
  432.0 16.3 %copy-start.4 = (bf16[272,2048]{1,0:T(8,128)(2,1)S(1)}, bf16[272,2048]{1,0:T(8,128)(2,1)}, u32[]{:S(2)}) copy-start(bf16[272,2048]{1,0:T(8,128)(2,1)} %fusion.174) | copy-start | bytes 3342340
  (44 other events, 118.2 us)
Sparse Core Ops, SparseCore 0:
  33.0 15.4 all-gather.8
  170.5 14.0 all-gather.4
  186.7 14.0 all-gather.10
  309.9 14.1 all-gather.6

commit v2 on v1

v2 whole, which is shorter than its diff:
```python
import functools
import math
import jax
import jax.numpy as jnp
from jax import lax
from jax.experimental import pallas as pl
from jax.experimental.pallas import tpu as pltpu
from jax.sharding import PartitionSpec as P

NORM_EPS = 1e-6
ROPE_THETA = 10000.0
NUM_LAYERS = 2
SWAP = [(0, 1), (1, 0)]
ROW_BLOCK = 16
MASKED = -1e30


def rope_tables(positions, head_dim):
    half_dim = head_dim // 2
    inv_freq = ROPE_THETA ** (-jnp.arange(half_dim, dtype=jnp.float32) * (2.0 / head_dim))
    angles = positions.astype(jnp.float32)[:, None] * inv_freq[None, :]
    return jnp.cos(angles), jnp.sin(angles)


def dot32(a, b):
    return jnp.dot(a, b, preferred_element_type=jnp.float32)


def f32(a):
    return a.astype(jnp.float32)


def bf16(a):
    return a.astype(jnp.bfloat16)


def gelu_tanh(x):
    return x * (0.5 * (1.0 + jnp.tanh(math.sqrt(2.0 / math.pi) * (x + 0.044715 * (x * x * x)))))


def add_parts(hidden, own, other):
    return bf16(f32(hidden) + f32(bf16(f32(own) + f32(other))))


def ds(start, size):
    return pl.ds(pl.multiple_of(start, size), size)


def norm_rows(parts, hid, gain, hid_out, x):
    scale = 1.0 + f32(gain[...])

    @pl.loop(0, hid.shape[0] // ROW_BLOCK)
    def _(blk):
        rows = ds(blk * ROW_BLOCK, ROW_BLOCK)
        h = hid[rows, :]
        if parts:
            h = add_parts(h, parts[0][rows, :], parts[1][rows, :])
            hid_out[rows, :] = h
        h = f32(h)
        x[rows, :] = bf16(h * lax.rsqrt(jnp.mean(h * h, axis=-1, keepdims=True) + NORM_EPS) * scale)


def attention_kernel(layer, has_parts, img_loc, *refs):
    parts, refs = (refs[:2], refs[2:]) if has_parts else ((), refs)
    hid, gain, cos, sin, length, wq, wk, wv, wo, *refs = refs
    hid_out, refs = (refs[0], refs[1:]) if has_parts else (None, refs)
    kv_out, part, x, kvs, q, o, wq_buf, wk_buf, wv_buf, wo_buf, wsem, send_sem, recv_sem = refs
    rows = hid.shape[0]
    head_dim = wk.shape[2]
    half = head_dim // 2
    heads = wq.shape[2] // head_dim
    txt_loc = rows - img_loc
    me = lax.axis_index("sp")
    core, chip = lax.bitwise_xor(me, 1), lax.bitwise_xor(me, 2)

    loads = [pltpu.make_async_copy(src.at[layer], dst, wsem.at[i]) for i, (src, dst) in enumerate(((wk, wk_buf), (wv, wv_buf), (wq, wq_buf), (wo, wo_buf)))]
    for load in loads:
        load.start()
    barrier = pltpu.get_barrier_semaphore()
    for peer in (core, chip):
        pl.semaphore_signal(barrier, inc=1, device_id={"sp": peer}, device_id_type=pl.DeviceIdType.MESH)

    norm_rows(parts, hid, gain, hid_out, x)

    def rope(v):
        first, second = v[:, :half], v[:, half:]
        return first * cos[...] - second * sin[...], second * cos[...] + first * sin[...]

    loads[0].wait()
    first, second = rope(dot32(x[...], wk_buf[...]))
    kvs[:rows, :half] = bf16(first)
    kvs[:rows, half:head_dim] = bf16(second)
    loads[1].wait()
    kvs[:rows, head_dim:] = bf16(dot32(x[...], wv_buf[...]))
    pl.semaphore_wait(barrier, 2)

    def send(i, src, dst, peer):
        return pltpu.make_async_remote_copy(src_ref=kvs.at[pl.ds(src * rows, rows)], dst_ref=kvs.at[pl.ds(dst * rows, rows)], send_sem=send_sem.at[i], recv_sem=recv_sem.at[i], device_id={"sp": peer}, device_id_type=pl.DeviceIdType.MESH)

    to_chip, to_core, relay = send(0, 0, 2, chip), send(1, 0, 1, core), send(2, 2, 3, core)
    to_chip.start()
    to_core.start()
    kv_out[...] = kvs[:rows, :]

    loads[2].wait()
    for head in range(heads):
        lanes = slice(head * head_dim, (head + 1) * head_dim)
        first, second = rope(dot32(x[...], wq_buf[:, lanes]))
        q[:, head * head_dim:head * head_dim + half] = bf16(bf16(first) * head_dim ** -0.5)
        q[:, head * head_dim + half:(head + 1) * head_dim] = bf16(bf16(second) * head_dim ** -0.5)

    to_chip.wait_recv()
    relay.start()
    col = lax.broadcasted_iota(jnp.int32, (1, 4 * rows), 1)
    slot = (col >= rows).astype(jnp.int32) + (col >= 2 * rows).astype(jnp.int32) + (col >= 3 * rows).astype(jnp.int32)
    idx = col - slot * rows
    owner = jnp.where(slot == 0, me, jnp.where(slot == 1, core, jnp.where(slot == 2, chip, lax.bitwise_xor(me, 3))))
    valid = (idx < img_loc) | (owner * txt_loc + idx - img_loc < length[0])
    to_core.wait_recv()
    relay.wait_recv()

    for head in range(heads):
        lanes = slice(head * head_dim, (head + 1) * head_dim)
        s = lax.dot_general(q[:, lanes], kvs[:, :head_dim], (((1,), (1,)), ((), ())), preferred_element_type=jnp.float32)
        s = jnp.where(valid, s, MASKED)
        e = jnp.exp(s - jnp.max(s, axis=-1, keepdims=True))
        p = bf16(e * (1.0 / jnp.sum(e, axis=-1, keepdims=True)))
        o[:, lanes] = bf16(dot32(p, kvs[:, head_dim:]))

    loads[3].wait()
    tile = 2 * head_dim
    for n in range(wo.shape[2] // tile):
        part[:, n * tile:(n + 1) * tile] = bf16(dot32(o[...], wo_buf[:, n * tile:(n + 1) * tile]))
    for copy in (to_chip, to_core, relay):
        copy.wait_send()


def attention(parts, hid, gain, cos, sin, length, wq, wk, wv, wo, layer, img_loc):
    rows, width = hid.shape
    qw, kw = wq.shape[2], wk.shape[2]
    vm = pl.BlockSpec(memory_space=pltpu.VMEM)
    anywhere = pl.BlockSpec(memory_space=pl.ANY)
    hid_shape = jax.ShapeDtypeStruct((rows, width), jnp.bfloat16)
    kv_shape = jax.ShapeDtypeStruct((rows, 2 * kw), jnp.bfloat16)
    outs = ((hid_shape,) if parts else ()) + (kv_shape, hid_shape)
    res = pl.pallas_call(
        functools.partial(attention_kernel, layer, bool(parts), img_loc),
        out_shape=outs,
        in_specs=[vm] * (len(parts) + 4) + [pl.BlockSpec(memory_space=pltpu.SMEM)] + [anywhere] * 4,
        out_specs=(vm,) * len(outs),
        scratch_shapes=[
            pltpu.VMEM((rows, width), jnp.bfloat16),
            pltpu.VMEM((4 * rows, 2 * kw), jnp.bfloat16),
            pltpu.VMEM((rows, qw), jnp.bfloat16),
            pltpu.VMEM((rows, qw), jnp.bfloat16),
            pltpu.VMEM((width, qw), jnp.bfloat16),
            pltpu.VMEM((width, kw), jnp.bfloat16),
            pltpu.VMEM((width, kw), jnp.bfloat16),
            pltpu.VMEM((qw, width), jnp.bfloat16),
            pltpu.SemaphoreType.DMA((4,)),
            pltpu.SemaphoreType.DMA((3,)),
            pltpu.SemaphoreType.DMA((3,)),
        ],
        compiler_params=pltpu.CompilerParams(collective_id=layer, has_side_effects=True, vmem_limit_bytes=40 << 20),
        cost_estimate=pl.CostEstimate(flops=12_000_000_000, bytes_accessed=2 * (2 * width * qw + 2 * width * kw), transcendentals=rows * rows * 16),
        name=f"attention{layer}",
    )(*parts, hid, gain, cos, sin, length, wq, wk, wv, wo)
    return res if parts else (hid, *res)


def mlp_kernel(layer, tf, tn, own, other, hid, gain, wg, wu, wd, hid_out, part, x, act, gbuf, ubuf, dbuf, gsem, usem, dsem):
    ff, width = wd.shape[1:]
    nf, nn = ff // tf, width // tn
    nb, nd = gbuf.shape[0], dbuf.shape[0]

    def load(src, buf, sem, tile, i, slot):
        return pltpu.make_async_copy(src.at[layer, :, ds(i * tile, tile)], buf.at[slot], sem.at[slot])

    gload = functools.partial(load, wg, gbuf, gsem, tf)
    uload = functools.partial(load, wu, ubuf, usem, tf)
    dload = functools.partial(load, wd, dbuf, dsem, tn)
    for i in range(nb):
        gload(i, i).start()
        uload(i, i).start()
    norm_rows((own, other), hid, gain, hid_out, x)

    @pl.loop(0, nf)
    def _(i):
        slot = lax.rem(i, nb)
        gload(i, slot).wait()
        gate = dot32(x[...], gbuf[slot])
        uload(i, slot).wait()
        act[:, ds(i * tf, tf)] = bf16(gelu_tanh(gate) * dot32(x[...], ubuf[slot]))

        @pl.when(i + nb < nf)
        def _():
            gload(i + nb, slot).start()
            uload(i + nb, slot).start()

        @pl.when((i + nb >= nf) & (i + nb < nf + nd))
        def _():
            dload(i + nb - nf, i + nb - nf).start()

    @pl.loop(0, nn)
    def _(i):
        slot = lax.rem(i, nd)
        dload(i, slot).wait()
        part[:, ds(i * tn, tn)] = bf16(dot32(act[...], dbuf[slot]))

        @pl.when(i + nd < nn)
        def _():
            dload(i + nd, slot).start()


def mlp(own, other, hid, gain, wg, wu, wd, layer, tf=1024, tn=512, nb=2, nd=2):
    rows, width = hid.shape
    ff = wg.shape[2]
    vm = pl.BlockSpec(memory_space=pltpu.VMEM)
    anywhere = pl.BlockSpec(memory_space=pl.ANY)
    hid_shape = jax.ShapeDtypeStruct((rows, width), jnp.bfloat16)
    return pl.pallas_call(
        functools.partial(mlp_kernel, layer, tf, tn),
        out_shape=(hid_shape, hid_shape),
        in_specs=[vm] * 4 + [anywhere] * 3,
        out_specs=(vm, vm),
        scratch_shapes=[
            pltpu.VMEM((rows, width), jnp.bfloat16),
            pltpu.VMEM((rows, ff), jnp.bfloat16),
            pltpu.VMEM((nb, width, tf), jnp.bfloat16),
            pltpu.VMEM((nb, width, tf), jnp.bfloat16),
            pltpu.VMEM((nd, ff, tn), jnp.bfloat16),
            pltpu.SemaphoreType.DMA((nb,)),
            pltpu.SemaphoreType.DMA((nb,)),
            pltpu.SemaphoreType.DMA((nd,)),
        ],
        compiler_params=pltpu.CompilerParams(vmem_limit_bytes=54 << 20),
        cost_estimate=pl.CostEstimate(flops=6 * rows * width * ff, bytes_accessed=6 * width * ff, transcendentals=rows * ff),
        name=f"mlp{layer}",
    )(own, other, hid, gain, wg, wu, wd)


def solution(mesh):
    sp_size = mesh.shape["sp"]
    in_specs = (P("dp", "sp", None), P("dp", "sp"), P("dp"), P(), P(), P("tp", None), P(), P(None, None, "tp"), P(), P(), P(None, "tp", None), P(), P(None, None, "tp"), P(None, None, "tp"), P(None, "tp", None))
    out_specs = (P("dp", "sp", None), P("dp", "sp", None), P(None, None, "dp", "sp", None), P(None, None, "dp", "sp", None))

    def device_fn(features, tokens, lengths, proj_w, proj_b, embed, ln_attn, w_query, w_key, w_value, w_out, ln_mlp, w_gate, w_up, w_down):
        num_req, img_loc, _ = features.shape
        txt_loc = tokens.shape[1]
        model_width = proj_w.shape[1]
        head_dim = w_key.shape[2]
        rows_loc = embed.shape[0]
        shard_idx = lax.axis_index("sp")
        tp_idx = lax.axis_index("tp")
        reqs = range(num_req)

        positions = jnp.concatenate([shard_idx * img_loc + jnp.arange(img_loc), img_loc * sp_size + shard_idx * txt_loc + jnp.arange(txt_loc)])
        cos_table, sin_table = rope_tables(positions, head_dim)

        hidden = []
        for req in reqs:
            local_ids = tokens[req] - tp_idx * rows_loc
            owned_row = (local_ids >= 0) & (local_ids < rows_loc)
            picked = jnp.take(embed, jnp.clip(local_ids, 0, rows_loc - 1), axis=0)
            picked = jnp.where(owned_row[:, None], picked, jnp.zeros((), jnp.bfloat16))
            txt_rows = bf16((f32(picked) + f32(lax.ppermute(picked, "tp", SWAP))) * math.sqrt(model_width))
            img_rows = bf16(dot32(features[req], proj_w) + f32(proj_b))
            hidden.append(jnp.concatenate([img_rows, txt_rows], axis=0))

        parts = [()] * num_req
        cache_parts = []
        for layer in range(NUM_LAYERS):
            kvs = [None] * num_req
            for req in reqs:
                hidden[req], kvs[req], part = attention(parts[req], hidden[req], ln_attn[layer:layer + 1], cos_table, sin_table, lengths[req:req + 1], w_query, w_key, w_value, w_out, layer, img_loc)
                parts[req] = (part, lax.ppermute(part, "tp", SWAP))
            for req in reqs:
                hidden[req], part = mlp(*parts[req], hidden[req], ln_mlp[layer:layer + 1], w_gate, w_up, w_down, layer)
                parts[req] = (part, lax.ppermute(part, "tp", SWAP))
            cache_parts.append(jnp.stack(kvs))
        cache = jnp.stack(cache_parts)
        cache = jnp.stack([cache[..., :head_dim], cache[..., head_dim:]], axis=1)
        hidden = jnp.stack([add_parts(hidden[req], *parts[req]) for req in reqs])
        return hidden[:, :img_loc], hidden[:, img_loc:], cache[:, :, :, :img_loc], cache[:, :, :, img_loc:]

    return jax.shard_map(device_fn, mesh=mesh, in_specs=in_specs, out_specs=out_specs, check_vma=False)
```

time: 463 us -> 318 us (0.69)
  matrix products: 268 us -> 5.58 us
  Pallas kernels: 0 us -> 224 us
  waiting for transfers between devices: 94.2 us -> 37.3 us
  other arithmetic: 40.7 us -> 10.8 us
  between operations: 15 us -> 1.26 us
    dot_general x46 -> x2, matrix products: 255 us -> 5.58 us  [dot32(): return jnp.dot(a, b, preferred_element_type=jnp.float32)]
    pallas_call x0 -> x8, Pallas kernels: none -> 224 us  [the longest x4 156 us: mlp(): pl.pallas_call(functools.partial(mlp_kernel, layer, tf, tn), out_shape=(h...]
    ppermute x10, waiting for transfers between devices: 83.7 us -> 37.3 us  [the longest x8 37.3 us: device_fn(): parts[req] = (part, lax.ppermute(part, 'tp', SWAP))]
    reduce_sum x24 -> x0, other arithmetic: 18.1 us -> none  [the longest x8 12.3 us: rms_norm(): mean_sq = jnp.mean(hid_f32 * hid_f32, axis=-1, keepdims=True)]
    dot_general x16 -> x0, matrix products: 12.6 us -> none  [device_fn(): lax.dot_general(query, kv_all[:, :head_dim], (((1,), (1,)), ((), ())), pr...]
    all_gather x4 -> x0, waiting for transfers between devices: 10.4 us -> none  [device_fn(): lax.all_gather(jnp.concatenate([key_rows, value_rows], axis=-1), 'sp', ax...]
    another operation x18 -> x8, other arithmetic: 12.9 us -> 3.56 us  [the longest x4 3.3 us: device_fn(): hidden = jnp.stack([add_parts(hidden[req], *parts[req]) for req in reqs])]
    unnamed x126 -> x64, local copies, waits for them, and re-layouts: 15.1 us -> 11.9 us
  transfers between devices with their start and end apart: 14 -> 10, of which waited for: 10 -> 4; matrix products, arithmetic and copies ran while one was open for 62% -> 6% of each run, Pallas kernels for 0% -> 72%
where the time goes in v2:
time: 318 us; the launch traced here: 313 us
  Pallas kernels  224 us (70%)
  waiting for transfers between devices  37.3 us (12%)
  local copies, waits for them, and re-layouts  22.1 us (7%)
  starting transfers between devices  12.1 us (4%)
  other arithmetic  10.8 us (3%)
  matrix products  5.58 us (2%)
    pallas_call x4, Pallas kernels, mlp(): pl.pallas_call(functools.partial(mlp_kernel, layer, tf, tn), out_shape=(h...  156 us
    pallas_call x4, Pallas kernels, attention(): pl.pallas_call(functools.partial(attention_kernel, layer, bool(parts), im...  68.1 us
    ppermute x8, waiting for transfers between devices, device_fn(): parts[req] = (part, lax.ppermute(part, 'tp', SWAP))  37.3 us
    unnamed x64, local copies, waits for them, and re-layouts  11.9 us
    gather x2, local copies, waits for them, and re-layouts, device_fn(): picked = jnp.take(embed, jnp.clip(local_ids, 0, rows_loc - 1), axis=0)  9.05 us
    ppermute x8, starting transfers between devices, device_fn(): parts[req] = (part, lax.ppermute(part, 'tp', SWAP))  8.76 us
  transfers between devices with their start and end apart: 10, of which 4 were waited for; matrix products, arithmetic and copies ran while one was open for 6% of the time, Pallas kernels for 72%

profile of v2, /device:TPU:0, one launch (start us, length us, event | category | flops | bytes accessed | tf_op | source)
XLA Modules:
  0.0 313.3 jit_solution(10199601937731903927)
XLA Ops:
  2.2 4.6 %gather_fusion = bf16[128,2048]{1,0:T(8,128)(2,1)S(1)} fusion(bf16[128000,2048]{1,0:T(8,128)(2,1)} %param.22, s32[1024]{0:T(1024)S(1)} %pad_clamp_fusion.1), kind=kCustom, calls=%fused_computation.clone | custom fusion | bytes 1049088 | tf_op jit(solution)/shard_map/jit(_take)/gather | solution.py:264
  7.7 3.3 %collective-permute-start = (bf16[128,2048]{1,0:T(8,128)(2,1)}, bf16[128,2048]{1,0:T(8,128)(2,1)}, u32[]{:S(2)}, u32[]{:S(2)}) collective-permute-start(bf16[128,2048]{1,0:T(8,128)(2,1)} %select_select_fusion.1), channel_id=1, source_target_pairs={{0,4},{4,0},{1,5},{5,1},{2,6},{6,2},{3,7},{7,3}} | collective-permute-start | bytes 1572872 | tf_op jit(solution)/shard_map/ppermute | solution.py:266
  11.0 4.5 %gather_fusion.1 = bf16[128,2048]{1,0:T(8,128)(2,1)S(1)} fusion(bf16[128000,2048]{1,0:T(8,128)(2,1)} %param.22, s32[1024]{0:T(1024)S(1)} %pad_clamp_fusion), kind=kCustom, calls=%fused_computation.1.clone | custom fusion | bytes 1049088 | tf_op jit(solution)/shard_map/jit(_take)/gather | solution.py:264
  16.6 4.0 %fusion.1 = bf16[144,2048]{1,0:T(8,128)(2,1)} fusion(bf16[1024,2048]{1,0:T(8,128)(2,1)} %param.20, f32[2048]{0:T(1024)S(1)} %convert_element_type.71, bf16[2,144,1024]{2,1,0:T(8,128)(2,1)S(1)} %copy-done.26), kind=kOutput, calls=%fused_computation.5 | convolution fusion | flops 604569600 | bytes 5087232 | tf_op jit(solution)/shard_map/dot_general | solution.py:26
  20.6 1.6 fusion
  24.1 1.5 multiply_convert_fusion.1
  25.7 1.9 copy-done.8
  27.6 16.7 %attention0.2 = (bf16[272,512]{1,0:T(8,128)(2,1)S(1)}, bf16[272,2048]{1,0:T(8,128)(2,1)S(1)}) custom-call(bf16[272,2048]{1,0:T(8,128)(2,1)S(1)} %pad_maximum_fusion.refs_0_.hid, bf16[1,2048]{1,0:T(2,128)(2,1)S(1)} %get-tuple-element.54.refs_1_, f32[272,128]{1,0:T(8,128)S(1)} %get-tuple-element.56.refs_2_.refs_4_, ...), custom_call_target="tpu_custom_call" | custom-call | flops 12000000000 | bytes 10485760 | tf_op jit(solution)/shard_map/attention0/pallas_call | solution.py:146
  44.3 1.8 collective-permute-start.1
  46.1 1.5 multiply_convert_fusion
  47.7 17.6 %attention0.3 = (bf16[272,512]{1,0:T(8,128)(2,1)S(1)}, bf16[272,2048]{1,0:T(8,128)(2,1)S(1)}) custom-call(bf16[272,2048]{1,0:T(8,128)(2,1)S(1)} %pad_maximum_fusion.1.refs_0_.hid, bf16[1,2048]{1,0:T(2,128)(2,1)S(1)} %get-tuple-element.54.refs_1_, f32[272,128]{1,0:T(8,128)S(1)} %get-tuple-element.56.refs_2_.refs_4_, ...), custom_call_target="tpu_custom_call" | custom-call | flops 12000000000 | bytes 10485760 | tf_op jit(solution)/shard_map/attention0/pallas_call | solution.py:146
  66.1 5.1 %collective-permute-done.1.other = bf16[272,2048]{1,0:T(8,128)(2,1)S(1)} collective-permute-done((bf16[272,2048]{1,0:T(8,128)(2,1)S(1)}, bf16[272,2048]{1,0:T(8,128)(2,1)S(1)}, u32[]{:S(2)}, u32[]{:S(2)}) %collective-permute-start.1) | collective-permute-done | bytes 1114144 | tf_op jit(solution)/shard_map/ppermute | solution.py:276
  71.2 1.1 copy-done.23
  72.2 39.3 %mlp0.2 = (bf16[272,2048]{1,0:T(8,128)(2,1)}, bf16[272,2048]{1,0:T(8,128)(2,1)}) custom-call(bf16[272,2048]{1,0:T(8,128)(2,1)} %copy-done.6, bf16[272,2048]{1,0:T(8,128)(2,1)} %copy-done.23, bf16[272,2048]{1,0:T(8,128)(2,1)} %copy-done, bf16[1,2048]{1,0:T(2,128)(2,1)} %get-tuple-element.52.gain, bf16[2,2048,8192]{2,1,0:T(8,128)(2,1)} %wg.7, ...), custom_call_target="tpu_custom_call" | custom-call | flops 27380416512 | bytes 100663296 | tf_op jit(solution)/shard_map/mlp0/pallas_call | solution.py:221
  111.6 2.0 collective-permute-start.2
  113.6 38.9 %mlp0.3 = (bf16[272,2048]{1,0:T(8,128)(2,1)}, bf16[272,2048]{1,0:T(8,128)(2,1)}) custom-call(bf16[272,2048]{1,0:T(8,128)(2,1)} %copy-done.7, bf16[272,2048]{1,0:T(8,128)(2,1)} %collective-permute-done.6.other, bf16[272,2048]{1,0:T(8,128)(2,1)} %copy-done.1, bf16[1,2048]{1,0:T(2,128)(2,1)} %get-tuple-element.52.gain, bf16[2,2048,8192]{2,1,0:T(8,128)(2,1)} %wg.7, ...), custom_call_target="tpu_custom_call" | custom-call | flops 27380416512 | bytes 100663296 | tf_op jit(solution)/shard_map/mlp0/pallas_call | solution.py:221
  152.7 1.0 copy-done.14
  153.7 1.2 copy-done.15
  154.9 17.8 %attention1.2 = (bf16[272,2048]{1,0:T(8,128)(2,1)S(1)}, bf16[272,512]{1,0:T(8,128)(2,1)S(1)}, bf16[272,2048]{1,0:T(8,128)(2,1)S(1)}) custom-call(bf16[272,2048]{1,0:T(8,128)(2,1)S(1)} %copy-done.13, bf16[272,2048]{1,0:T(8,128)(2,1)S(1)} %copy-done.15, bf16[272,2048]{1,0:T(8,128)(2,1)S(1)} %copy-done.12, bf16[1,2048]{1,0:T(2,128)(2,1)S(1)} %get-tuple-element.53.refs_3_, ...), custom_call_target="tpu_custom_call" | custom-call | flops 12000000000 | bytes 10485760 | tf_op jit(solution)/shard_map/attention1/pallas_call | solution.py:146
  172.8 1.0 copy-done.2
  173.8 2.0 collective-permute-start.3
  175.7 4.2 %collective-permute-done.7.refs_1_ = bf16[272,2048]{1,0:T(8,128)(2,1)S(1)} collective-permute-done((bf16[272,2048]{1,0:T(8,128)(2,1)}, bf16[272,2048]{1,0:T(8,128)(2,1)S(1)}, u32[]{:S(2)}, u32[]{:S(2)}) %collective-permute-start.7) | collective-permute-done | bytes 1114144 | tf_op jit(solution)/shard_map/ppermute | solution.py:279
  179.9 15.9 %attention1.3 = (bf16[272,2048]{1,0:T(8,128)(2,1)S(1)}, bf16[272,512]{1,0:T(8,128)(2,1)S(1)}, bf16[272,2048]{1,0:T(8,128)(2,1)S(1)}) custom-call(bf16[272,2048]{1,0:T(8,128)(2,1)S(1)} %copy-done.11, bf16[272,2048]{1,0:T(8,128)(2,1)S(1)} %collective-permute-done.7.refs_1_, bf16[272,2048]{1,0:T(8,128)(2,1)S(1)} %copy-done.10, ...), custom_call_target="tpu_custom_call" | custom-call | flops 12000000000 | bytes 10485760 | tf_op jit(solution)/shard_map/attention1/pallas_call | solution.py:146
  195.8 1.0 copy-done.4
  196.9 6.9 %collective-permute-done.3.other = bf16[272,2048]{1,0:T(8,128)(2,1)S(1)} collective-permute-done((bf16[272,2048]{1,0:T(8,128)(2,1)S(1)}, bf16[272,2048]{1,0:T(8,128)(2,1)S(1)}, u32[]{:S(2)}, u32[]{:S(2)}) %collective-permute-start.3) | collective-permute-done | bytes 1114144 | tf_op jit(solution)/shard_map/ppermute | solution.py:276
  203.8 1.0 copy-done.24
  204.8 39.0 %mlp1.2 = (bf16[272,2048]{1,0:T(8,128)(2,1)}, bf16[272,2048]{1,0:T(8,128)(2,1)}) custom-call(bf16[272,2048]{1,0:T(8,128)(2,1)} %copy-done.3, bf16[272,2048]{1,0:T(8,128)(2,1)} %copy-done.24, bf16[272,2048]{1,0:T(8,128)(2,1)} %copy-done.2, bf16[1,2048]{1,0:T(2,128)(2,1)} %get-tuple-element.51.gain, bf16[2,2048,8192]{2,1,0:T(8,128)(2,1)} %wg.7, ...), custom_call_target="tpu_custom_call" | custom-call | flops 27380416512 | bytes 100663296 | tf_op jit(solution)/shard_map/mlp1/pallas_call | solution.py:221
  245.0 38.8 %mlp1.3 = (bf16[272,2048]{1,0:T(8,128)(2,1)}, bf16[272,2048]{1,0:T(8,128)(2,1)}) custom-call(bf16[272,2048]{1,0:T(8,128)(2,1)} %copy-done.5, bf16[272,2048]{1,0:T(8,128)(2,1)} %copy-done.25, bf16[272,2048]{1,0:T(8,128)(2,1)} %copy-done.4, bf16[1,2048]{1,0:T(2,128)(2,1)} %get-tuple-element.51.gain, bf16[2,2048,8192]{2,1,0:T(8,128)(2,1)} %wg.7, ...), custom_call_target="tpu_custom_call" | custom-call | flops 27380416512 | bytes 100663296 | tf_op jit(solution)/shard_map/mlp1/pallas_call | solution.py:221
  283.8 1.9 collective-permute-start.9
  289.2 21.1 %collective-permute-done.9 = bf16[272,2048]{1,0:T(8,128)(2,1)S(1)} collective-permute-done((bf16[272,2048]{1,0:T(8,128)(2,1)}, bf16[272,2048]{1,0:T(8,128)(2,1)S(1)}, u32[]{:S(2)}, u32[]{:S(2)}) %collective-permute-start.9) | collective-permute-done | bytes 1114144 | tf_op jit(solution)/shard_map/ppermute | solution.py:279
  310.9 1.0 pad_maximum_fusion.2
  311.9 1.1 fusion.2
  (91 shorter events, 11.7 us)
Async XLA Ops:
  7.7 16.4 %collective-permute-start = (bf16[128,2048]{1,0:T(8,128)(2,1)}, bf16[128,2048]{1,0:T(8,128)(2,1)}, u32[]{:S(2)}, u32[]{:S(2)}) collective-permute-start(bf16[128,2048]{1,0:T(8,128)(2,1)} %select_select_fusion.1), channel_id=1, source_target_pairs={{0,4},{4,0},{1,5},{5,1},{2,6},{6,2},{3,7},{7,3}} | collective-permute-start | bytes 1572872 | tf_op jit(solution)/shard_map/ppermute | solution.py:266
  11.0 5.6 %copy-start.29 = (bf16[2048]{0:T(1024)(128)(2,1)S(1)}, bf16[2048]{0:T(1024)(128)(2,1)}, u32[]{:S(2)}) copy-start(bf16[2048]{0:T(1024)(128)(2,1)} %param.21) | copy-start | bytes 12292
  16.4 29.7 %collective-permute-start.5 = (bf16[128,2048]{1,0:T(8,128)(2,1)}, bf16[128,2048]{1,0:T(8,128)(2,1)}, u32[]{:S(2)}, u32[]{:S(2)}) collective-permute-start(bf16[128,2048]{1,0:T(8,128)(2,1)} %select_select_fusion), channel_id=1, source_target_pairs={{0,4},{4,0},{1,5},{5,1},{2,6},{6,2},{3,7},{7,3}} | collective-permute-start | bytes 1572872 | tf_op jit(solution)/shard_map/ppermute | solution.py:266
  16.6 4.0 %copy-start.16 = (bf16[1024,2048]{1,0:T(8,128)(2,1)S(1)}, bf16[1024,2048]{1,0:T(8,128)(2,1)}, u32[]{:S(2)}) copy-start(bf16[1024,2048]{1,0:T(8,128)(2,1)} %param.20) | copy-start | bytes 12582916
  20.5 1.7 copy-start.27
  20.5 2.3 copy-start.30
  20.6 2.9 copy-start.28
  20.6 5.1 %copy-start.9 = (bf16[2,2048,256]{2,1,0:T(8,128)(2,1)S(1)}, bf16[2,2048,256]{2,1,0:T(8,128)(2,1)}, u32[]{:S(2)}) copy-start(bf16[2,2048,256]{2,1,0:T(8,128)(2,1)} %refs_9_.3) | copy-start | bytes 6291460
  22.2 3.4 %copy-start.18 = (bf16[144,2048]{1,0:T(8,128)(2,1)S(1)}, bf16[144,2048]{1,0:T(8,128)(2,1)}, u32[]{:S(2)}) copy-start(bf16[144,2048]{1,0:T(8,128)(2,1)} %fusion) | copy-start | bytes 1769476
  25.6 2.0 copy-start.8
  25.7 18.6 %copy-start = (bf16[272,2048]{1,0:T(8,128)(2,1)}, bf16[272,2048]{1,0:T(8,128)(2,1)S(1)}, u32[]{:S(2)}) copy-start(bf16[272,2048]{1,0:T(8,128)(2,1)S(1)} %pad_maximum_fusion.refs_0_.hid) | copy-start | bytes 3342340
  44.3 3.5 %copy-start.6 = (bf16[272,2048]{1,0:T(8,128)(2,1)}, bf16[272,2048]{1,0:T(8,128)(2,1)S(1)}, u32[]{:S(2)}) copy-start(bf16[272,2048]{1,0:T(8,128)(2,1)S(1)} %get-tuple-element.23.own) | copy-start | bytes 3342340
  44.3 3.3 %copy-start.17 = (bf16[144,2048]{1,0:T(8,128)(2,1)S(1)}, bf16[144,2048]{1,0:T(8,128)(2,1)}, u32[]{:S(2)}) copy-start(bf16[144,2048]{1,0:T(8,128)(2,1)} %fusion.1) | copy-start | bytes 1769476
  44.3 26.9 %collective-permute-start.1 = (bf16[272,2048]{1,0:T(8,128)(2,1)S(1)}, bf16[272,2048]{1,0:T(8,128)(2,1)S(1)}, u32[]{:S(2)}, u32[]{:S(2)}) collective-permute-start(bf16[272,2048]{1,0:T(8,128)(2,1)S(1)} %get-tuple-element.23.own), channel_id=1, source_target_pairs={{0,4},{4,0},{1,5},{5,1},{2,6},{6,2},{3,7},{7,3}} | collective-permute-start | bytes 3342344 | tf_op jit(solution)/shard_map/ppermute | solution.py:276
  47.7 17.7 %copy-start.1 = (bf16[272,2048]{1,0:T(8,128)(2,1)}, bf16[272,2048]{1,0:T(8,128)(2,1)S(1)}, u32[]{:S(2)}) copy-start(bf16[272,2048]{1,0:T(8,128)(2,1)S(1)} %pad_maximum_fusion.1.refs_0_.hid) | copy-start | bytes 3342340
  65.4 46.2 %copy-start.7 = (bf16[272,2048]{1,0:T(8,128)(2,1)}, bf16[272,2048]{1,0:T(8,128)(2,1)S(1)}, u32[]{:S(2)}) copy-start(bf16[272,2048]{1,0:T(8,128)(2,1)S(1)} %get-tuple-element.30.own) | copy-start | bytes 3342340
  65.4 48.2 %collective-permute-start.6 = (bf16[272,2048]{1,0:T(8,128)(2,1)S(1)}, bf16[272,2048]{1,0:T(8,128)(2,1)}, u32[]{:S(2)}, u32[]{:S(2)}) collective-permute-start(bf16[272,2048]{1,0:T(8,128)(2,1)S(1)} %get-tuple-element.30.own), channel_id=1, source_target_pairs={{0,4},{4,0},{1,5},{5,1},{2,6},{6,2},{3,7},{7,3}} | collective-permute-start | bytes 3342344 | tf_op jit(solution)/shard_map/ppermute | solution.py:276
  111.6 42.1 %copy-start.12 = (bf16[272,2048]{1,0:T(8,128)(2,1)S(1)}, bf16[272,2048]{1,0:T(8,128)(2,1)}, u32[]{:S(2)}) copy-start(bf16[272,2048]{1,0:T(8,128)(2,1)} %get-tuple-element.25.refs_2_) | copy-start | bytes 3342340
  111.6 42.1 %copy-start.13 = (bf16[272,2048]{1,0:T(8,128)(2,1)S(1)}, bf16[272,2048]{1,0:T(8,128)(2,1)}, u32[]{:S(2)}) copy-start(bf16[272,2048]{1,0:T(8,128)(2,1)} %get-tuple-element.24.refs_0_) | copy-start | bytes 3342340
  111.6 41.1 %collective-permute-start.2 = (bf16[272,2048]{1,0:T(8,128)(2,1)}, bf16[272,2048]{1,0:T(8,128)(2,1)S(1)}, u32[]{:S(2)}, u32[]{:S(2)}) collective-permute-start(bf16[272,2048]{1,0:T(8,128)(2,1)} %get-tuple-element.24.refs_0_), channel_id=1, source_target_pairs={{0,4},{4,0},{1,5},{5,1},{2,6},{6,2},{3,7},{7,3}} | collective-permute-start | bytes 3342344 | tf_op jit(solution)/shard_map/ppermute | solution.py:279
  152.5 27.5 %collective-permute-start.7 = (bf16[272,2048]{1,0:T(8,128)(2,1)}, bf16[272,2048]{1,0:T(8,128)(2,1)S(1)}, u32[]{:S(2)}, u32[]{:S(2)}) collective-permute-start(bf16[272,2048]{1,0:T(8,128)(2,1)} %get-tuple-element.31.refs_0_), channel_id=1, source_target_pairs={{0,4},{4,0},{1,5},{5,1},{2,6},{6,2},{3,7},{7,3}} | collective-permute-start | bytes 3342344 | tf_op jit(solution)/shard_map/ppermute | solution.py:279
  154.9 25.0 %copy-start.10 = (bf16[272,2048]{1,0:T(8,128)(2,1)S(1)}, bf16[272,2048]{1,0:T(8,128)(2,1)}, u32[]{:S(2)}) copy-start(bf16[272,2048]{1,0:T(8,128)(2,1)} %get-tuple-element.32.refs_2_) | copy-start | bytes 3342340
  154.9 25.0 %copy-start.11 = (bf16[272,2048]{1,0:T(8,128)(2,1)S(1)}, bf16[272,2048]{1,0:T(8,128)(2,1)}, u32[]{:S(2)}) copy-start(bf16[272,2048]{1,0:T(8,128)(2,1)} %get-tuple-element.31.refs_0_) | copy-start | bytes 3342340
  173.8 22.0 %copy-start.3 = (bf16[272,2048]{1,0:T(8,128)(2,1)}, bf16[272,2048]{1,0:T(8,128)(2,1)S(1)}, u32[]{:S(2)}) copy-start(bf16[272,2048]{1,0:T(8,128)(2,1)S(1)} %get-tuple-element.26.own) | copy-start | bytes 3342340
  173.8 30.0 %collective-permute-start.3 = (bf16[272,2048]{1,0:T(8,128)(2,1)S(1)}, bf16[272,2048]{1,0:T(8,128)(2,1)S(1)}, u32[]{:S(2)}, u32[]{:S(2)}) collective-permute-start(bf16[272,2048]{1,0:T(8,128)(2,1)S(1)} %get-tuple-element.26.own), channel_id=1, source_target_pairs={{0,4},{4,0},{1,5},{5,1},{2,6},{6,2},{3,7},{7,3}} | collective-permute-start | bytes 3342344 | tf_op jit(solution)/shard_map/ppermute | solution.py:276
  196.8 47.0 %copy-start.5 = (bf16[272,2048]{1,0:T(8,128)(2,1)}, bf16[272,2048]{1,0:T(8,128)(2,1)S(1)}, u32[]{:S(2)}) copy-start(bf16[272,2048]{1,0:T(8,128)(2,1)S(1)} %get-tuple-element.33.own) | copy-start | bytes 3342340
  196.8 47.1 %collective-permute-start.8 = (bf16[272,2048]{1,0:T(8,128)(2,1)S(1)}, bf16[272,2048]{1,0:T(8,128)(2,1)S(1)}, u32[]{:S(2)}, u32[]{:S(2)}) collective-permute-start(bf16[272,2048]{1,0:T(8,128)(2,1)S(1)} %get-tuple-element.33.own), channel_id=1, source_target_pairs={{0,4},{4,0},{1,5},{5,1},{2,6},{6,2},{3,7},{7,3}} | collective-permute-start | bytes 3342344 | tf_op jit(solution)/shard_map/ppermute | solution.py:276
  243.8 43.9 %collective-permute-start.4 = (bf16[272,2048]{1,0:T(8,128)(2,1)}, bf16[272,2048]{1,0:T(8,128)(2,1)S(1)}, u32[]{:S(2)}, u32[]{:S(2)}) collective-permute-start(bf16[272,2048]{1,0:T(8,128)(2,1)} %get-tuple-element.29), channel_id=1, source_target_pairs={{0,4},{4,0},{1,5},{5,1},{2,6},{6,2},{3,7},{7,3}} | collective-permute-start | bytes 3342344 | tf_op jit(solution)/shard_map/ppermute | solution.py:279
  283.8 26.5 %collective-permute-start.9 = (bf16[272,2048]{1,0:T(8,128)(2,1)}, bf16[272,2048]{1,0:T(8,128)(2,1)S(1)}, u32[]{:S(2)}, u32[]{:S(2)}) collective-permute-start(bf16[272,2048]{1,0:T(8,128)(2,1)} %get-tuple-element.36), channel_id=1, source_target_pairs={{0,4},{4,0},{1,5},{5,1},{2,6},{6,2},{3,7},{7,3}} | collective-permute-start | bytes 3342344 | tf_op jit(solution)/shard_map/ppermute | solution.py:279
  286.8 1.8 copy-start.20
  288.6 21.7 %copy-start.21 = (bf16[272,2048]{1,0:T(8,128)(2,1)S(1)}, bf16[272,2048]{1,0:T(8,128)(2,1)}, u32[]{:S(2)}) copy-start(bf16[272,2048]{1,0:T(8,128)(2,1)} %get-tuple-element.35) | copy-start | bytes 3342340
  288.6 21.7 %copy-start.22 = (bf16[272,2048]{1,0:T(8,128)(2,1)S(1)}, bf16[272,2048]{1,0:T(8,128)(2,1)}, u32[]{:S(2)}) copy-start(bf16[272,2048]{1,0:T(8,128)(2,1)} %get-tuple-element.36) | copy-start | bytes 3342340
  (9 other events, 9.9 us)

commit v3 on v0

v3 whole, which is shorter than its diff:
```python
import functools
import math
import numpy as np
import jax
import jax.numpy as jnp
from jax import lax
from jax.experimental import pallas as pl
from jax.experimental.pallas import tpu as pltpu
from jax.sharding import PartitionSpec as P

NORM_EPS = 1e-6
ROPE_THETA = 10000.0
NUM_LAYERS = 2
NUM_REQ = 2
BLOCK = 16
GROUP = 8
MASKED = -1e30
MESH_ID = pl.DeviceIdType.MESH
VMEM_SPEC = pl.BlockSpec(memory_space=pltpu.VMEM)
SMEM_SPEC = pl.BlockSpec(memory_space=pltpu.SMEM)
ANY_SPEC = pl.BlockSpec(memory_space=pl.ANY)
DMA = pltpu.SemaphoreType.DMA


def vmem(*shape):
    return pltpu.VMEM(shape, jnp.bfloat16)


def out(*shape):
    return jax.ShapeDtypeStruct(shape, jnp.bfloat16)


def dot32(a, b):
    return jnp.dot(a, b, preferred_element_type=jnp.float32)


def f32(a):
    return a.astype(jnp.float32)


def bf16(a):
    return a.astype(jnp.bfloat16)


def gelu_tanh(x):
    return x * (0.5 * (1.0 + jnp.tanh(math.sqrt(2.0 / math.pi) * (x + 0.044715 * (x * x * x)))))


def add_parts(hidden, own, other):
    return bf16(f32(hidden) + f32(bf16(f32(own) + f32(other))))


def normed(h, scale):
    h = f32(h)
    return bf16(h * lax.rsqrt(jnp.mean(h * h, axis=-1, keepdims=True) + NORM_EPS) * scale)


def ds(start, size, multiple=None):
    return pl.ds(pl.multiple_of(start, multiple or size), size)


def each_block(rows, body):
    @pl.loop(0, rows // BLOCK)
    def _(blk):
        body(lambda base: ds(base + blk * BLOCK, BLOCK))


def greet(peers):
    barrier = pltpu.get_barrier_semaphore()
    for peer in peers:
        pl.semaphore_signal(barrier, inc=1, device_id=peer, device_id_type=MESH_ID)
    pl.semaphore_wait(barrier, len(peers))


def remote(src, dst, send_sem, recv_sem, peer):
    return pltpu.make_async_remote_copy(src_ref=src, dst_ref=dst, send_sem=send_sem, recv_sem=recv_sem, device_id=peer, device_id_type=MESH_ID)


def start_kernel(ids, id_col, features, bias, proj, embed, img, picked, groups, proj_buf, gsem, psem):
    rows_loc = embed.shape[0]
    num = ids.shape[0]
    lo = lax.axis_index("tp") * rows_loc
    load = pltpu.make_async_copy(proj, proj_buf, psem)

    def fetch(i, row):
        return pltpu.make_async_copy(embed.at[ds(row, GROUP)], groups.at[i], gsem)

    @pl.loop(0, num)
    def _(i):
        row = jnp.clip(ids[i] - lo, 0, rows_loc - 1)
        fetch(i, row - lax.rem(row, GROUP)).start()

    load.start()
    load.wait()
    tile = 512
    for n in range(proj.shape[1] // tile):
        cols = slice(n * tile, (n + 1) * tile)
        img[:, cols] = bf16(dot32(features[...], proj_buf[:, cols]) + f32(bias[:, cols]))

    pltpu.make_async_copy(groups, groups, gsem).wait()

    part = 64
    sub = lax.broadcasted_iota(jnp.int32, (part, part * GROUP), 0)
    col = lax.broadcasted_iota(jnp.int32, (part, part * GROUP), 1)
    for p in range(num // part):
        rel = id_col[p * part:(p + 1) * part, :] - lo
        want = jnp.where((rel >= 0) & (rel < rows_loc), rel & (GROUP - 1), -GROUP * part * 2)
        pick = jnp.where(col == sub * GROUP + want, 1.0, 0.0).astype(jnp.bfloat16)
        rows = groups[p * part:(p + 1) * part].reshape(part * GROUP, groups.shape[2])
        picked[p * part:(p + 1) * part, :] = bf16(dot32(pick, rows))


def start(tokens, features, proj_w, proj_b, embed):
    num = tokens.size
    vis, width = proj_w.shape
    feats = features.reshape(-1, vis)
    return pl.pallas_call(
        start_kernel,
        out_shape=(out(feats.shape[0], width), out(num, width)),
        in_specs=[SMEM_SPEC, VMEM_SPEC, VMEM_SPEC, VMEM_SPEC, ANY_SPEC, ANY_SPEC],
        out_specs=(VMEM_SPEC, VMEM_SPEC),
        scratch_shapes=[vmem(num, GROUP, width), vmem(vis, width), DMA, DMA],
        compiler_params=pltpu.CompilerParams(vmem_limit_bytes=32 << 20),
        name="start",
    )(tokens.reshape(num), tokens.reshape(num, 1), feats, proj_b.reshape(1, width), proj_w, embed)


def attention_kernel(layer, img_loc, *refs):
    first = layer == 0
    refs, refs_in = (refs[2:], refs[:2]) if first else (refs[4:], refs[:4])
    gain, cos, sin, lengths, wq, wk, wv, wo, hid, kv, part, recv, x, arrive, kvs, q, o, wq_buf, wk_buf, wv_buf, wo_buf, wsem, tp_send, tp_recv, sp_send, sp_recv = refs
    rows = hid.shape[0] // NUM_REQ
    txt_loc = rows - img_loc
    head_dim = wk.shape[2]
    half = head_dim // 2
    heads = wq.shape[2] // head_dim
    width = hid.shape[1]
    me = lax.axis_index("sp")
    twin = {"tp": 1 - lax.axis_index("tp")}
    near, far, cross = [lax.bitwise_xor(me, k) for k in (1, 2, 3)]

    loads = [pltpu.make_async_copy(src.at[layer], dst, wsem.at[i]) for i, (src, dst) in enumerate(((wk, wk_buf), (wv, wv_buf), (wq, wq_buf), (wo, wo_buf)))]
    loads[0].start()
    loads[1].start()
    greet(({"sp": near}, {"sp": far}, twin))
    if first:
        img, picked = refs_in
        span = [pl.ds(req * txt_loc, txt_loc) for req in range(NUM_REQ)]
        arrivals = [remote(picked.at[span[req]], arrive.at[span[req]], tp_send.at[req], tp_recv.at[req], twin) for req in range(NUM_REQ)]
    else:
        hid_in, mlp_part, mlp_recv, mlp_tile = refs_in
        done = mlp_tile.shape[1]
        arrivals = [None, remote(mlp_part.at[pl.ds(rows, rows), pl.ds(done, width - done)], arrive.at[:, pl.ds(done, width - done)], tp_send.at[1], tp_recv.at[1], twin)]
    for arrival in arrivals:
        if arrival is not None:
            arrival.start()
    scale = 1.0 + f32(gain[...])

    def keep(at, local, h):
        hid[at, :] = h
        x[local, :] = normed(h, scale)

    def embedded(req):
        def image(at):
            keep(at(req * rows), at(0), img[at(req * img_loc), :])

        def prompt(at):
            src = at(req * txt_loc)
            keep(at(req * rows + img_loc), at(img_loc), bf16((f32(picked[src, :]) + f32(arrive[src, :])) * math.sqrt(width)))

        each_block(img_loc, image)
        arrivals[req].wait_recv()
        each_block(txt_loc, prompt)

    def continued(req):
        other = mlp_recv if req == 0 else arrive
        if req == 1:
            arrive[:, :done] = mlp_tile[...]
            arrivals[1].wait_recv()

        def row_block(at):
            src = at(req * rows)
            keep(src, at(0), add_parts(hid_in[src, :], mlp_part[src, :], other[at(0), :]))

        each_block(rows, row_block)

    def rope(v):
        a, b = v[:, :half], v[:, half:]
        return a * cos[...] - b * sin[...], b * cos[...] + a * sin[...]

    def before(req):
        (embedded if first else continued)(req)
        slots = [pl.ds((req * 4 + k) * rows, rows) for k in range(4)]
        if req == 0:
            loads[0].wait()
            loads[2].start()
            loads[3].start()
        a, b = rope(dot32(x[...], wk_buf[...]))
        kvs[slots[0], :half] = bf16(a)
        kvs[slots[0], half:head_dim] = bf16(b)
        if req == 0:
            loads[1].wait()
        kvs[slots[0], head_dim:] = bf16(dot32(x[...], wv_buf[...]))
        sends = [remote(kvs.at[slots[src]], kvs.at[slots[dst]], sp_send.at[req * 3 + i], sp_recv.at[req * 3 + i], {"sp": peer}) for i, (src, dst, peer) in enumerate(((0, 2, far), (0, 1, near), (2, 3, near)))]
        sends[0].start()
        sends[1].start()
        kv[pl.ds(req * rows, rows), :] = kvs[slots[0], :]
        if req == 0:
            loads[2].wait()
        for head in range(heads):
            base = head * head_dim
            a, b = rope(dot32(x[...], wq_buf[:, base:base + head_dim]))
            q[:, base:base + half] = bf16(bf16(a) * head_dim ** -0.5)
            q[:, base + half:base + head_dim] = bf16(bf16(b) * head_dim ** -0.5)
        return sends

    col = lax.broadcasted_iota(jnp.int32, (1, 4 * rows), 1)
    slot = (col >= rows).astype(jnp.int32) + (col >= 2 * rows).astype(jnp.int32) + (col >= 3 * rows).astype(jnp.int32)
    owner = jnp.where(slot == 0, me, jnp.where(slot == 1, near, jnp.where(slot == 2, far, cross)))
    idx = col - slot * rows
    text_pos = jnp.where(idx < img_loc, -1, owner * txt_loc + idx - img_loc)

    def after(req, sends):
        sends[0].wait_recv()
        sends[2].start()
        sends[1].wait_recv()
        sends[2].wait_recv()
        valid = text_pos < lengths[req]
        every = pl.ds(req * 4 * rows, 4 * rows)
        for head in range(heads):
            lanes = slice(head * head_dim, (head + 1) * head_dim)
            s = lax.dot_general(q[:, lanes], kvs[every, :head_dim], (((1,), (1,)), ((), ())), preferred_element_type=jnp.float32)
            s = jnp.where(valid, s, MASKED)
            e = jnp.exp(s - jnp.max(s, axis=-1, keepdims=True))
            p = bf16(e * (1.0 / jnp.sum(e, axis=-1, keepdims=True)))
            o[:, lanes] = bf16(dot32(p, kvs[every, head_dim:]))
        if req == 0:
            loads[3].wait()
        tile = 2 * head_dim
        for n in range(width // tile):
            cols = slice(n * tile, (n + 1) * tile)
            part[pl.ds(req * rows, rows), cols] = bf16(dot32(o[...], wo_buf[:, cols]))

    swap = remote(part.at[pl.ds(0, rows)], recv, tp_send.at[2], tp_recv.at[2], twin)
    sends = before(0)
    after(0, sends)
    swap.start()
    more = before(1)
    after(1, more)
    swap.wait_recv()
    for copy in (*sends, *more, *[a for a in arrivals if a is not None], swap):
        copy.wait_send()


def attention(sources, gain, cos, sin, lengths, wq, wk, wv, wo, layer, img_loc):
    rows = cos.shape[0]
    width, qw = wq.shape[1:]
    kw = wk.shape[2]
    arrive_rows = sources[1].shape[0] if layer == 0 else rows
    return pl.pallas_call(
        functools.partial(attention_kernel, layer, img_loc),
        out_shape=(out(NUM_REQ * rows, width), out(NUM_REQ * rows, 2 * kw), out(NUM_REQ * rows, width), out(rows, width)),
        in_specs=[VMEM_SPEC] * (len(sources) + 3) + [SMEM_SPEC] + [ANY_SPEC] * 4,
        out_specs=(VMEM_SPEC,) * 4,
        scratch_shapes=[
            vmem(rows, width), vmem(arrive_rows, width), vmem(NUM_REQ * 4 * rows, 2 * kw), vmem(rows, qw), vmem(rows, qw),
            vmem(width, qw), vmem(width, kw), vmem(width, kw), vmem(qw, width),
            DMA((4,)), DMA((3,)), DMA((3,)), DMA((6,)), DMA((6,)),
        ],
        compiler_params=pltpu.CompilerParams(collective_id=layer, has_side_effects=True, vmem_limit_bytes=48 << 20),
        name=f"attention{layer}",
    )(*sources, gain, cos, sin, lengths, wq, wk, wv, wo)


def mlp_kernel(layer, img_loc, tf, tn, hid_in, own, recv0, gain, wg, wu, wd, *refs):
    last = layer == NUM_LAYERS - 1
    if last:
        image, prompt, hid, part, recv, tiles, *refs = refs
    else:
        hid, part, recv, tiles, *refs = refs
    other, x, act, gbuf, ubuf, dbuf, gsem, usem, dsem, tp_send, tp_recv = refs
    rows = recv0.shape[0]
    ff, width = wd.shape[1:]
    nf, nn = ff // tf, width // tn
    nb, nd = gbuf.shape[0], dbuf.shape[0]
    streamed = nn if last else 1
    twin = {"tp": 1 - lax.axis_index("tp")}

    def load(src, buf, sem, tile, i, slot):
        return pltpu.make_async_copy(src.at[layer, :, ds(i * tile, tile)], buf.at[slot], sem.at[slot])

    gload = functools.partial(load, wg, gbuf, gsem, tf)
    uload = functools.partial(load, wu, ubuf, usem, tf)
    dload = functools.partial(load, wd, dbuf, dsem, tn)
    for i in range(nb):
        gload(i, i).start()
        uload(i, i).start()
    greet((twin,))
    upper = pl.ds(rows, rows)
    incoming = remote(own.at[upper], other.at[upper], tp_send.at[0], tp_recv.at[0], twin)
    incoming.start()
    swap = remote(part.at[pl.ds(0, rows)], recv, tp_send.at[1], tp_recv.at[1], twin)

    def stream(n):
        cols = ds(n * tn, tn)
        return remote(part.at[upper, cols], tiles.at[:, cols], tp_send.at[2 + n], tp_recv.at[2 + n], twin)

    def bring(at):
        other[at(0), :] = recv0[at(0), :]

    each_block(rows, bring)
    scale = 1.0 + f32(gain[...])

    @pl.loop(0, NUM_REQ)
    def _(req):
        @pl.when(req == 1)
        def _():
            incoming.wait_recv()

        def row_block(at):
            src = at(req * rows)
            h = add_parts(hid_in[src, :], own[src, :], other[src, :])
            hid[src, :] = h
            x[at(0), :] = normed(h, scale)

        each_block(rows, row_block)

        @pl.loop(0, nf)
        def _(i):
            slot = lax.rem(i, nb)
            gload(i, slot).wait()
            gate = dot32(x[...], gbuf[slot])
            uload(i, slot).wait()
            act[:, ds(i * tf, tf)] = bf16(gelu_tanh(gate) * dot32(x[...], ubuf[slot]))

            @pl.when(i + nb < nf)
            def _():
                gload(i + nb, slot).start()
                uload(i + nb, slot).start()

            @pl.when((i + nb >= nf) & (i + nb < nf + nd))
            def _():
                dload(i + nb - nf, i + nb - nf).start()

        @pl.loop(0, nn)
        def _(i):
            slot = lax.rem(i, nd)
            dload(i, slot).wait()
            part[ds(req * rows, rows, BLOCK), ds(i * tn, tn)] = bf16(dot32(act[...], dbuf[slot]))

            @pl.when(i + nd < nn)
            def _():
                dload(i + nd, slot).start()

            @pl.when((i + nd >= nn) & (req == 0))
            def _():
                gload(i + nd - nn, i + nd - nn).start()
                uload(i + nd - nn, i + nd - nn).start()

            @pl.when((req == 1) & (i < streamed))
            def _():
                stream(i).start()

        @pl.when(req == 0)
        def _():
            swap.start()

    swap.wait_recv()
    if last:
        def finish(req, others, at_other, cols):
            def image_block(at):
                src = at(req * rows)
                image[req, at(0), cols] = add_parts(hid[src, cols], part[src, cols], others[at(0), at_other])

            def prompt_block(at):
                src = at(req * rows + img_loc)
                prompt[req, at(0), cols] = add_parts(hid[src, cols], part[src, cols], others[at(img_loc), at_other])

            each_block(img_loc, image_block)
            each_block(rows - img_loc, prompt_block)

        finish(0, recv, slice(None), slice(None))
        for n in range(nn):
            cols = pl.ds(n * tn, tn)
            stream(n).wait_recv()
            finish(1, tiles, cols, cols)
    else:
        stream(0).wait_recv()
    incoming.wait_send()
    swap.wait_send()
    for n in range(streamed):
        stream(n).wait_send()


def mlp(hid, own, recv, gain, wg, wu, wd, layer, img_loc, tf=1024, tn=512, nb=2, nd=2):
    rows, width = recv.shape
    ff = wg.shape[2]
    last = layer == NUM_LAYERS - 1
    if last:
        outs = (out(NUM_REQ, img_loc, width), out(NUM_REQ, rows - img_loc, width))
        extra = [vmem(NUM_REQ * rows, width), vmem(NUM_REQ * rows, width), vmem(rows, width), vmem(rows, width)]
    else:
        outs = (out(NUM_REQ * rows, width), out(NUM_REQ * rows, width), out(rows, width), out(rows, tn))
        extra = []
    return pl.pallas_call(
        functools.partial(mlp_kernel, layer, img_loc, tf, tn),
        out_shape=outs,
        in_specs=[VMEM_SPEC] * 4 + [ANY_SPEC] * 3,
        out_specs=(VMEM_SPEC,) * len(outs),
        scratch_shapes=extra + [
            vmem(NUM_REQ * rows, width), vmem(rows, width), vmem(rows, ff),
            vmem(nb, width, tf), vmem(nb, width, tf), vmem(nd, ff, tn),
            DMA((nb,)), DMA((nb,)), DMA((nd,)), DMA((2 + width // tn,)), DMA((2 + width // tn,)),
        ],
        compiler_params=pltpu.CompilerParams(collective_id=NUM_LAYERS + layer, has_side_effects=True, vmem_limit_bytes=63 << 20),
        name=f"mlp{layer}",
    )(hid, own, recv, gain, wg, wu, wd)


def solution(mesh):
    sp_size = mesh.shape["sp"]
    in_specs = (P("dp", "sp", None), P("dp", "sp"), P("dp"), P(), P(), P("tp", None), P(), P(None, None, "tp"), P(), P(), P(None, "tp", None), P(), P(None, None, "tp"), P(None, None, "tp"), P(None, "tp", None))
    out_specs = (P("dp", "sp", None), P("dp", "sp", None), P(None, None, "dp", "sp", None), P(None, None, "dp", "sp", None))

    def device_fn(features, tokens, lengths, proj_w, proj_b, embed, ln_attn, w_query, w_key, w_value, w_out, ln_mlp, w_gate, w_up, w_down):
        img_loc, txt_loc = features.shape[1], tokens.shape[1]
        rows = img_loc + txt_loc
        head_dim = w_key.shape[2]
        shard_idx = lax.axis_index("sp")
        local = jnp.arange(rows)
        positions = jnp.where(local < img_loc, shard_idx * img_loc + local, img_loc * sp_size + shard_idx * txt_loc + local - img_loc)
        inv_freq = np.power(np.float32(ROPE_THETA), -np.arange(head_dim // 2, dtype=np.float32) * np.float32(2.0 / head_dim))
        angles = f32(positions)[:, None] * inv_freq[None, :]
        cos, sin = jnp.cos(angles), jnp.sin(angles)

        sources = start(tokens, features, proj_w, proj_b, embed)
        caches = []
        for layer in range(NUM_LAYERS):
            hid, kv, part, recv = attention(sources, ln_attn[layer:layer + 1], cos, sin, lengths, w_query, w_key, w_value, w_out, layer, img_loc)
            caches.append(kv.reshape(NUM_REQ, rows, 2, head_dim))
            sources = mlp(hid, part, recv, ln_mlp[layer:layer + 1], w_gate, w_up, w_down, layer, img_loc)
        cache = jnp.stack(caches).transpose(0, 3, 1, 2, 4)
        return *sources, cache[:, :, :, :img_loc], cache[:, :, :, img_loc:]

    return jax.shard_map(device_fn, mesh=mesh, in_specs=in_specs, out_specs=out_specs, check_vma=False)
```

time: 581 us -> 312 us (0.54)
  Pallas kernels: 0 us -> 289 us
  waiting for transfers between devices: 277 us -> 0 us
  matrix products: 208 us -> 0 us
  other arithmetic: 36.7 us -> 1.33 us
  local copies, waits for them, and re-layouts: 36.1 us -> 20 us
  between operations: 14.8 us -> 0.8 us
    pallas_call x0 -> x5, Pallas kernels: none -> 289 us  [the longest x2 172 us: mlp(): pl.pallas_call(functools.partial(mlp_kernel, layer, img_loc, tf, tn), out...]
    psum x5 -> x0, waiting for transfers between devices: 269 us -> none  [the longest x2 119 us: device_fn(): lax.psum(attn_part, 'tp').astype(jnp.float32)]
    dot_general x17 -> x0, matrix products: 208 us -> none  [the longest x2 56.4 us: device_fn(): jnp.einsum('bsd,df->bsf', normed, w_up[layer_idx], preferred_element_type...]
    dot_general x3 -> x0, local copies, waits for them, and re-layouts: 19 us -> none  [device_fn(): jnp.einsum('bsd,dn->bsn', normed, w_query[layer_idx], preferred_element_t...]
    unnamed x62 -> x26, local copies, waits for them, and re-layouts: 0.39 us -> 12.5 us
    reduce_sum x4 -> x0, other arithmetic: 11.3 us -> none  [rms_norm(): mean_sq = jnp.mean(hid_f32 * hid_f32, axis=-1, keepdims=True)]
    sub x3 -> x0, other arithmetic: 11 us -> none  [the longest x2 11 us: device_fn(): attn_probs = jax.nn.softmax(scores, axis=-1).astype(jnp.bfloat16)]
    all_gather x2 -> x0, waiting for transfers between devices: 7.94 us -> none  [device_fn(): lax.all_gather(jnp.concatenate([key_rows, value_rows], axis=-1), 'sp', ax...]
  transfers between devices with their start and end apart: 7 -> 0, of which waited for: 6 -> 0; matrix products, arithmetic and copies ran while one was open for 7% -> 0% of each run, Pallas kernels for 0% -> 0%
where the time goes in v3:
time: 312 us; the launch traced here: 311 us
  Pallas kernels  289 us (93%)
  local copies, waits for them, and re-layouts  20 us (6%)
    pallas_call x2, Pallas kernels, mlp(): pl.pallas_call(functools.partial(mlp_kernel, layer, img_loc, tf, tn), out...  172 us
    pallas_call x2, Pallas kernels, attention(): pl.pallas_call(functools.partial(attention_kernel, layer, img_loc), out_s...  108 us
    unnamed x26, local copies, waits for them, and re-layouts  12.5 us
    pallas_call x1, Pallas kernels, start(): pl.pallas_call(start_kernel, out_shape=(out(feats.shape[0], width), out(n...  8.73 us

profile of v3, /device:TPU:0, one launch (start us, length us, event | category | flops | bytes accessed | tf_op | source)
XLA Modules:
  0.0 311.1 jit_solution(17140035358269052144)
XLA Ops:
  0.6 0.7 reshape.34.bias
  1.3 0.8 fusion.1
  2.1 1.4 fusion
  3.5 0.8 copy.22.id_col
  4.3 1.2 multiply_sine_fusion
  5.6 0.0 copy-start.1
  5.6 2.2 copy-done.1
  7.8 1.1 copy-done.5
  8.8 0.7 copy-done.8
  9.5 8.7 %start.1 = (bf16[288,2048]{1,0:T(8,128)(2,1)S(1)}, bf16[256,2048]{1,0:T(8,128)(2,1)S(1)}) custom-call(s32[256]{0:T(256)S(1)} %bitcast.7, s32[256,1]{1,0:T(8,128)S(1)} %copy.22.id_col, bf16[288,1024]{1,0:T(8,128)(2,1)S(1)} %bitcast.5, bf16[1,2048]{1,0:T(2,128)(2,1)S(1)} %reshape.34.bias, bf16[1024,2048]{1,0:T(8,128)(2,1)S(1)} %copy-done.1, ...), custom_call_target="tpu_custom_call" | custom-call | tf_op jit(solution)/shard_map/start/pallas_call | solution.py:117
  18.2 59.4 %attention0.1 = (bf16[544,2048]{1,0:T(8,128)(2,1)}, bf16[544,512]{1,0:T(8,128)(2,1)S(1)}, bf16[544,2048]{1,0:T(8,128)(2,1)}, bf16[272,2048]{1,0:T(8,128)(2,1)S(1)}) custom-call(bf16[288,2048]{1,0:T(8,128)(2,1)S(1)} %get-tuple-element.20.refs_0_, bf16[256,2048]{1,0:T(8,128)(2,1)S(1)} %get-tuple-element.21.refs_1_, ...), custom_call_target="tpu_custom_call" | custom-call | tf_op jit(solution)/shard_map/attention0/pallas_call | solution.py:260
  77.6 0.0 copy-start.4
  77.7 1.0 copy-done.4
  78.6 77.5 %mlp0.1 = (bf16[544,2048]{1,0:T(8,128)(2,1)}, bf16[544,2048]{1,0:T(8,128)(2,1)}, bf16[272,2048]{1,0:T(8,128)(2,1)}, bf16[272,512]{1,0:T(8,128)(2,1)}) custom-call(bf16[544,2048]{1,0:T(8,128)(2,1)} %get-tuple-element.22.hid_in, bf16[544,2048]{1,0:T(8,128)(2,1)} %get-tuple-element.23.own, bf16[272,2048]{1,0:T(8,128)(2,1)} %copy-done.4, ...), custom_call_target="tpu_custom_call" | custom-call | tf_op jit(solution)/shard_map/mlp0/pallas_call | solution.py:405
  156.2 0.0 copy-start
  156.2 1.6 copy-done
  157.8 1.2 copy-done.2
  159.0 1.0 copy-done.7
  160.0 49.1 %attention1.1 = (bf16[544,2048]{1,0:T(8,128)(2,1)}, bf16[544,512]{1,0:T(8,128)(2,1)S(1)}, bf16[544,2048]{1,0:T(8,128)(2,1)}, bf16[272,2048]{1,0:T(8,128)(2,1)S(1)}) custom-call(bf16[544,2048]{1,0:T(8,128)(2,1)} %get-tuple-element.25.refs_0_, bf16[544,2048]{1,0:T(8,128)(2,1)} %get-tuple-element.26.refs_1_, bf16[272,2048]{1,0:T(8,128)(2,1)S(1)} %copy-done.2, ...), custom_call_target="tpu_custom_call" | custom-call | tf_op jit(solution)/shard_map/attention1/pallas_call | solution.py:260
  209.0 0.0 copy-start.3
  209.1 1.0 copy-done.3
  210.0 0.8 copy-done.6
  210.8 94.3 %mlp1.1 = (bf16[2,144,2048]{2,1,0:T(8,128)(2,1)}, bf16[2,128,2048]{2,1,0:T(8,128)(2,1)}) custom-call(bf16[544,2048]{1,0:T(8,128)(2,1)} %get-tuple-element.29.hid_in, bf16[544,2048]{1,0:T(8,128)(2,1)} %get-tuple-element.30.own, bf16[272,2048]{1,0:T(8,128)(2,1)} %copy-done.3, bf16[1,2048]{1,0:T(2,128)(2,1)} %get-tuple-element.36.gain, ...), custom_call_target="tpu_custom_call" | custom-call | tf_op jit(solution)/shard_map/mlp1/pallas_call | solution.py:405
  305.1 1.9 stack_reshape.7
  307.0 0.1 copy.24
  307.1 0.1 stack_reshape.6
  307.3 0.1 copy.23
  307.3 0.1 maximum_bitcast_fusion
  307.5 0.8 slice.25
  308.3 0.9 slice.24
  309.2 1.0 copy.27
  310.2 1.0 copy.28
  (12 shorter events, 0.0 us)
Async XLA Ops:
  5.6 2.2 copy-start.1
  7.8 1.1 copy-start.5
  8.8 0.7 copy-start.8
  9.5 8.7 %copy-start.9 = (s32[2]{0:T(128)S(1)}, s32[2]{0:T(128)}, u32[]{:S(2)}) copy-start(s32[2]{0:T(128)} %refs_7_.3) | copy-start | bytes 28
  77.6 1.0 copy-start.4
  156.2 1.6 copy-start
  157.8 1.2 copy-start.2
  159.0 1.0 copy-start.7
  209.0 1.0 copy-start.3
  210.0 0.8 copy-start.6
  307.3 1.8 copy-start.10
  307.5 2.7 copy-start.11

commit v4 on v3

v4 whole, which is shorter than its diff:
```python
import functools
import math
import numpy as np
import jax
import jax.numpy as jnp
from jax import lax
from jax.experimental import pallas as pl
from jax.experimental.pallas import tpu as pltpu
from jax.sharding import PartitionSpec as P

NORM_EPS = 1e-6
ROPE_THETA = 10000.0
NUM_LAYERS = 2
NUM_REQ = 2
BLOCK = 16
GROUP = 8
MASKED = -1e30
MESH_ID = pl.DeviceIdType.MESH
VMEM_SPEC = pl.BlockSpec(memory_space=pltpu.VMEM)
SMEM_SPEC = pl.BlockSpec(memory_space=pltpu.SMEM)
ANY_SPEC = pl.BlockSpec(memory_space=pl.ANY)
HBM_SPEC = pl.BlockSpec(memory_space=pltpu.HBM)
DMA = pltpu.SemaphoreType.DMA


def vmem(*shape):
    return pltpu.VMEM(shape, jnp.bfloat16)


def out(*shape):
    return jax.ShapeDtypeStruct(shape, jnp.bfloat16)


def dot32(a, b):
    return jnp.dot(a, b, preferred_element_type=jnp.float32)


def f32(a):
    return a.astype(jnp.float32)


def bf16(a):
    return a.astype(jnp.bfloat16)


def gelu_tanh(x):
    return x * (0.5 * (1.0 + jnp.tanh(math.sqrt(2.0 / math.pi) * (x + 0.044715 * (x * x * x)))))


def add_parts(hidden, own, other):
    return bf16(f32(hidden) + f32(bf16(f32(own) + f32(other))))


def normed(h, scale):
    h = f32(h)
    return bf16(h * lax.rsqrt(jnp.mean(h * h, axis=-1, keepdims=True) + NORM_EPS) * scale)


def ds(start, size, multiple=None):
    return pl.ds(pl.multiple_of(start, multiple or size), size)


def each_block(rows, body):
    @pl.loop(0, rows // BLOCK)
    def _(blk):
        body(lambda base: ds(base + blk * BLOCK, BLOCK))


def greet(peers):
    barrier = pltpu.get_barrier_semaphore()
    for peer in peers:
        pl.semaphore_signal(barrier, inc=1, device_id=peer, device_id_type=MESH_ID)
    pl.semaphore_wait(barrier, len(peers))


def remote(src, dst, send_sem, recv_sem, peer):
    return pltpu.make_async_remote_copy(src_ref=src, dst_ref=dst, send_sem=send_sem, recv_sem=recv_sem, device_id=peer, device_id_type=MESH_ID)


def start_kernel(ids, id_rows, embed, picked, groups, sem):
    rows_loc = embed.shape[0]
    num = id_rows.shape[1]
    lo = lax.axis_index("tp") * rows_loc
    for req in range(NUM_REQ):
        @pl.loop(0, num, unroll=8)
        def _(i):
            row = jnp.clip(ids[req, i] - lo, 0, rows_loc - 1)
            pltpu.make_async_copy(embed.at[ds(row - (row & (GROUP - 1)), GROUP)], groups.at[req * num + i], sem.at[req]).start()

    line = lax.broadcasted_iota(jnp.int32, (num * GROUP, num), 0)
    lane = lax.broadcasted_iota(jnp.int32, (num * GROUP, num), 1)
    for req in range(NUM_REQ):
        rel = id_rows[req:req + 1, :] - lo
        want = jnp.where((rel >= 0) & (rel < rows_loc), rel & (GROUP - 1), -GROUP * num)
        pick = jnp.where(line - lane * GROUP == want, 1.0, 0.0).astype(jnp.bfloat16)
        mine = groups.at[pl.ds(req * num, num)]
        pltpu.make_async_copy(mine, mine, sem.at[req]).wait()
        rows = mine[...].reshape(num * GROUP, groups.shape[2])
        picked[req * num:(req + 1) * num, :] = bf16(lax.dot_general(pick, rows, (((0,), (0,)), ((), ())), preferred_element_type=jnp.float32))


def start(tokens, embed):
    num, width = tokens.size, embed.shape[1]
    return pl.pallas_call(
        start_kernel,
        out_shape=out(num, width),
        in_specs=[SMEM_SPEC, VMEM_SPEC, ANY_SPEC],
        out_specs=VMEM_SPEC,
        scratch_shapes=[vmem(num, GROUP, width), DMA((NUM_REQ,))],
        compiler_params=pltpu.CompilerParams(vmem_limit_bytes=32 << 20),
        name="start",
    )(tokens, tokens, embed)


def attention_kernel(layer, img_loc, *refs):
    first = layer == 0
    if first:
        picked, features, proj, bias, *refs = refs
    else:
        hid_in, mlp_part, mlp_recv, mlp_tile, kv_before, *refs = refs
    gain, freq, lengths, wq, wk, wv, wo, hid_out, part_out, recv, *refs = refs
    if first:
        kv, *refs = refs
    else:
        cache_image, cache_prompt, *refs = refs
    hid, part, x, arrive, kvs, q, o, cos, sin, wq_buf, wk_buf, wv_buf, wo_buf, lsem, osem, tp_send, tp_recv, sp_send, sp_recv, *refs = refs
    rows = hid.shape[0] // NUM_REQ
    txt_loc = rows - img_loc
    head_dim = wk.shape[2]
    half = head_dim // 2
    heads = wq.shape[2] // head_dim
    width = hid.shape[1]
    me = lax.axis_index("sp")
    twin = {"tp": 1 - lax.axis_index("tp")}
    near, far, cross = [lax.bitwise_xor(me, k) for k in (1, 2, 3)]
    pieces = ((0, img_loc), (img_loc, txt_loc)) if first else ((0, rows),)

    def load(i, src, dst):
        return pltpu.make_async_copy(src, dst, lsem.at[i])

    weights = [load(i, src.at[layer], dst) for i, (src, dst) in enumerate(((wk, wk_buf), (wv, wv_buf), (wq, wq_buf), (wo, wo_buf)))]
    if first:
        feat_buf, proj_buf = refs
        inputs = [load(4 + req, features.at[req], feat_buf.at[req]) for req in range(NUM_REQ)] + [load(6, proj, proj_buf)]
    else:
        own, other = refs
        done = mlp_tile.shape[1]
        lower, upper = pl.ds(0, rows), pl.ds(rows, rows)
        inputs = [load(4, hid_in.at[lower], hid.at[lower]), load(5, mlp_part.at[lower], own.at[lower]), load(6, mlp_recv, other), load(7, hid_in.at[upper], hid.at[upper]), load(8, mlp_part.at[upper], own.at[upper]), load(9, mlp_tile, arrive.at[:, pl.ds(0, done)])]
    for copy in (*inputs[:3], *weights, *inputs[3:]):
        copy.start()
    greet(({"sp": near}, {"sp": far}, twin))
    if first:
        span = [pl.ds(req * txt_loc, txt_loc) for req in range(NUM_REQ)]
        arrivals = [remote(picked.at[span[req]], arrive.at[span[req]], tp_send.at[req], tp_recv.at[req], twin) for req in range(NUM_REQ)]
    else:
        rest = pl.ds(done, width - done)
        arrivals = [remote(mlp_part.at[upper, rest], arrive.at[:, rest], tp_send.at[1], tp_recv.at[1], twin)]
    for arrival in arrivals:
        arrival.start()
    scale = 1.0 + f32(gain[layer:layer + 1, :])

    local = lax.broadcasted_iota(jnp.int32, (rows, half), 0)
    position = jnp.where(local < img_loc, me * img_loc + local, img_loc * 4 + me * txt_loc + local - img_loc)
    angles = f32(position) * freq[...]
    cos[...] = jnp.cos(angles)
    sin[...] = jnp.sin(angles)

    def rope(v, at):
        a, b = v[:, :half], v[:, half:]
        return a * cos[at, :] - b * sin[at, :], b * cos[at, :] + a * sin[at, :]

    def slot(req, k, lo, size):
        return pl.ds((req * 4 + k) * rows + lo, size)

    def sends(req, p):
        lo, size = pieces[p]
        base = (req * len(pieces) + p) * 3
        return [remote(kvs.at[slot(req, src, lo, size)], kvs.at[slot(req, dst, lo, size)], sp_send.at[base + i], sp_recv.at[base + i], {"sp": peer}) for i, (src, dst, peer) in enumerate(((0, 2, far), (0, 1, near), (2, 3, near)))]

    waited = set()

    def once(i):
        if i not in waited:
            waited.add(i)
            weights[i].wait()

    def project(req, p):
        lo, size = pieces[p]
        at = pl.ds(lo, size)
        here = pl.ds(req * rows + lo, size)
        mine = slot(req, 0, lo, size)
        once(0)
        a, b = rope(dot32(x[here, :], wk_buf[...]), at)
        kvs[mine, :half] = bf16(a)
        kvs[mine, half:head_dim] = bf16(b)
        once(1)
        kvs[mine, head_dim:] = bf16(dot32(x[here, :], wv_buf[...]))
        to_far, to_near, _ = sends(req, p)
        to_far.start()
        to_near.start()
        if first:
            kv[here, :] = kvs[mine, :]
        else:
            for j in range(2):
                lanes = pl.ds(j * head_dim, head_dim)
                for src, base in ((kv_before, req * rows), (kvs, req * 4 * rows)):
                    dst = 0 if src is kv_before else 1
                    cache_image[dst, j, req] = src[pl.ds(base, img_loc), lanes]
                    cache_prompt[dst, j, req] = src[pl.ds(base + img_loc, txt_loc), lanes]
        once(2)
        for head in range(heads):
            base = head * head_dim
            a, b = rope(dot32(x[here, :], wq_buf[:, base:base + head_dim]), at)
            q[here, base:base + half] = bf16(bf16(a) * head_dim ** -0.5)
            q[here, base + half:base + head_dim] = bf16(bf16(b) * head_dim ** -0.5)

    col = lax.broadcasted_iota(jnp.int32, (1, 4 * rows), 1)
    slot_of = (col >= rows).astype(jnp.int32) + (col >= 2 * rows).astype(jnp.int32) + (col >= 3 * rows).astype(jnp.int32)
    owner = jnp.where(slot_of == 0, me, jnp.where(slot_of == 1, near, jnp.where(slot_of == 2, far, cross)))
    idx = col - slot_of * rows
    text_pos = jnp.where(idx < img_loc, -1, owner * txt_loc + idx - img_loc)

    def attend(req):
        for p in range(len(pieces)):
            to_far, _, relay = sends(req, p)
            to_far.wait_recv()
            relay.start()
        for p in range(len(pieces)):
            _, to_near, relay = sends(req, p)
            to_near.wait_recv()
            relay.wait_recv()
        valid = text_pos < lengths[req]
        every = pl.ds(req * 4 * rows, 4 * rows)
        here = pl.ds(req * rows, rows)
        for head in range(heads):
            lanes = slice(head * head_dim, (head + 1) * head_dim)
            s = lax.dot_general(q[here, lanes], kvs[every, :head_dim], (((1,), (1,)), ((), ())), preferred_element_type=jnp.float32)
            s = jnp.where(valid, s, MASKED)
            e = jnp.exp(s - jnp.max(s, axis=-1, keepdims=True))
            p = bf16(e * (1.0 / jnp.sum(e, axis=-1, keepdims=True)))
            o[:, lanes] = bf16(dot32(p, kvs[every, head_dim:]))
        once(3)
        tile = 2 * head_dim
        for n in range(width // tile):
            cols = slice(n * tile, (n + 1) * tile)
            part[here, cols] = bf16(dot32(o[...], wo_buf[:, cols]))

    def put(i, src, dst, req):
        here = pl.ds(req * rows, rows)
        return pltpu.make_async_copy(src.at[here], dst.at[here], osem.at[i])

    puts = [put(2 * req + i, src, dst, req) for req in range(NUM_REQ) for i, (src, dst) in enumerate(((hid, hid_out), (part, part_out)))]
    swap = remote(part.at[pl.ds(0, rows)], recv, tp_send.at[2], tp_recv.at[2], twin)

    def keep(at, h):
        hid[at, :] = h
        x[at, :] = normed(h, scale)

    if first:
        for copy in inputs:
            copy.wait()
        for req in range(NUM_REQ):
            for n in range(4):
                cols = slice(n * (width // 4), (n + 1) * (width // 4))
                hid[pl.ds(req * rows, img_loc), cols] = bf16(dot32(feat_buf[req], proj_buf[:, cols]) + f32(bias[cols]).reshape(1, width // 4))

            def image(at):
                src = at(req * rows)
                x[src, :] = normed(hid[src, :], scale)

            each_block(img_loc, image)
            project(req, 0)

    for req in range(NUM_REQ):
        if first:
            arrivals[req].wait_recv()

            def prompt(at):
                src = at(req * txt_loc)
                keep(at(req * rows + img_loc), bf16((f32(picked[src, :]) + f32(arrive[src, :])) * math.sqrt(width)))

            each_block(txt_loc, prompt)
            puts[2 * req].start()
            project(req, 1)
        else:
            for copy in inputs[3 * req:3 * req + 3]:
                copy.wait()
            if req == 1:
                arrivals[0].wait_recv()
            incoming = other if req == 0 else arrive

            def row_block(at):
                src = at(req * rows)
                keep(src, add_parts(hid[src, :], own[src, :], incoming[at(0), :]))

            each_block(rows, row_block)
            puts[2 * req].start()
            project(req, 0)
        attend(req)
        puts[2 * req + 1].start()
        if req == 0:
            swap.start()
    for copy in puts:
        copy.wait()
    swap.wait_recv()
    for copy in (*arrivals, swap, *[c for req in range(NUM_REQ) for p in range(len(pieces)) for c in sends(req, p)]):
        copy.wait_send()


def attention(sources, extra, gain, freq, lengths, wq, wk, wv, wo, layer, rows, img_loc):
    width, qw = wq.shape[1:]
    kw = wk.shape[2]
    txt_loc = rows - img_loc
    total = NUM_REQ * rows
    first = layer == 0
    if first:
        specs = [VMEM_SPEC, HBM_SPEC, HBM_SPEC, VMEM_SPEC]
        outs, out_specs = (out(total, 2 * kw),), (VMEM_SPEC,)
        scratch = [vmem(NUM_REQ, img_loc, extra[0].shape[2]), vmem(*extra[1].shape)]
    else:
        specs = [HBM_SPEC] * 4 + [VMEM_SPEC]
        outs, out_specs = tuple(out(NUM_LAYERS, 2, NUM_REQ, n, kw) for n in (img_loc, txt_loc)), (VMEM_SPEC, VMEM_SPEC)
        scratch = [vmem(total, width), vmem(rows, width)]
    copies = NUM_REQ * 3 * (2 if first else 1)
    return pl.pallas_call(
        functools.partial(attention_kernel, layer, img_loc),
        out_shape=(out(total, width), out(total, width), out(rows, width), *outs),
        in_specs=specs + [VMEM_SPEC] * 2 + [SMEM_SPEC] + [ANY_SPEC] * 4,
        out_specs=(HBM_SPEC,) * 3 + out_specs,
        scratch_shapes=[
            vmem(total, width), vmem(total, width), vmem(total, width), vmem(NUM_REQ * txt_loc if first else rows, width),
            vmem(NUM_REQ * 4 * rows, 2 * kw), vmem(total, qw), vmem(rows, qw),
            pltpu.VMEM((rows, kw // 2), jnp.float32), pltpu.VMEM((rows, kw // 2), jnp.float32),
            vmem(width, qw), vmem(width, kw), vmem(width, kw), vmem(qw, width),
            DMA((10,)), DMA((2 * NUM_REQ,)), DMA((3,)), DMA((3,)), DMA((copies,)), DMA((copies,)), *scratch,
        ],
        compiler_params=pltpu.CompilerParams(collective_id=layer, has_side_effects=True, vmem_limit_bytes=56 << 20),
        name=f"attention{layer}",
    )(*sources, *extra, gain, freq, lengths, wq, wk, wv, wo)


def mlp_kernel(layer, img_loc, tf, tn, hid_in, own_in, recv0, gain, wg, wu, wd, *refs):
    last = layer == NUM_LAYERS - 1
    if last:
        image, prompt, recv, tiles, *refs = refs
    else:
        hid_out, part_out, recv, tiles, *refs = refs
    hid, own, part, other, x, act, gbuf, ubuf, dbuf, lsem, osem, gsem, usem, dsem, tp_send, tp_recv = refs
    rows = recv0.shape[0]
    lower, upper = pl.ds(0, rows), pl.ds(rows, rows)
    inputs = [pltpu.make_async_copy(src, dst, lsem.at[i]) for i, (src, dst) in enumerate(((hid_in.at[lower], hid.at[lower]), (own_in.at[lower], own.at[lower]), (recv0, other.at[lower]), (hid_in.at[upper], hid.at[upper]), (own_in.at[upper], own.at[upper])))]
    for copy in inputs:
        copy.start()
    ff, width = wd.shape[1:]
    nf, nn = ff // tf, width // tn
    nb, nd = gbuf.shape[0], dbuf.shape[0]
    streamed = nn if last else 1
    twin = {"tp": 1 - lax.axis_index("tp")}

    def load(src, buf, sem, tile, i, slot):
        return pltpu.make_async_copy(src.at[layer, :, ds(i * tile, tile)], buf.at[slot], sem.at[slot])

    gload = functools.partial(load, wg, gbuf, gsem, tf)
    uload = functools.partial(load, wu, ubuf, usem, tf)
    dload = functools.partial(load, wd, dbuf, dsem, tn)
    for i in range(nb):
        gload(i, i).start()
        uload(i, i).start()
    greet((twin,))
    incoming = remote(own_in.at[upper], other.at[upper], tp_send.at[0], tp_recv.at[0], twin)
    incoming.start()
    swap = remote(part.at[lower], recv, tp_send.at[1], tp_recv.at[1], twin)

    def stream(n):
        cols = ds(n * tn, tn)
        return remote(part.at[upper, cols], tiles.at[:, cols], tp_send.at[2 + n], tp_recv.at[2 + n], twin)

    scale = 1.0 + f32(gain[layer:layer + 1, :])
    for copy in inputs:
        copy.wait()

    def put(i, src, dst, req):
        here = ds(req * rows, rows, BLOCK)
        return pltpu.make_async_copy(src.at[here], dst.at[here], osem.at[2 * req + i])

    @pl.loop(0, NUM_REQ)
    def _(req):
        @pl.when(req == 1)
        def _():
            incoming.wait_recv()

        def row_block(at):
            src = at(req * rows)
            h = add_parts(hid[src, :], own[src, :], other[src, :])
            hid[src, :] = h
            x[at(0), :] = normed(h, scale)

        each_block(rows, row_block)
        if not last:
            put(0, hid, hid_out, req).start()

        @pl.loop(0, nf)
        def _(i):
            slot = lax.rem(i, nb)
            gload(i, slot).wait()
            gate = dot32(x[...], gbuf[slot])
            uload(i, slot).wait()
            act[:, ds(i * tf, tf)] = bf16(gelu_tanh(gate) * dot32(x[...], ubuf[slot]))

            @pl.when(i + nb < nf)
            def _():
                gload(i + nb, slot).start()
                uload(i + nb, slot).start()

            @pl.when((i + nb >= nf) & (i + nb < nf + nd))
            def _():
                dload(i + nb - nf, i + nb - nf).start()

        @pl.loop(0, nn)
        def _(i):
            slot = lax.rem(i, nd)
            dload(i, slot).wait()
            part[ds(req * rows, rows, BLOCK), ds(i * tn, tn)] = bf16(dot32(act[...], dbuf[slot]))

            @pl.when(i + nd < nn)
            def _():
                dload(i + nd, slot).start()

            @pl.when((i + nd >= nn) & (req == 0))
            def _():
                gload(i + nd - nn, i + nd - nn).start()
                uload(i + nd - nn, i + nd - nn).start()

            @pl.when((req == 1) & (i < streamed))
            def _():
                stream(i).start()

        if not last:
            put(1, part, part_out, req).start()

        @pl.when(req == 0)
        def _():
            swap.start()

    swap.wait_recv()
    if last:
        def finish(req, others, at_other, cols):
            def image_block(at):
                src = at(req * rows)
                image[req, at(0), cols] = add_parts(hid[src, cols], part[src, cols], others[at(0), at_other])

            def prompt_block(at):
                src = at(req * rows + img_loc)
                prompt[req, at(0), cols] = add_parts(hid[src, cols], part[src, cols], others[at(img_loc), at_other])

            each_block(img_loc, image_block)
            each_block(rows - img_loc, prompt_block)

        finish(0, recv, slice(None), slice(None))
        for n in range(nn):
            cols = pl.ds(n * tn, tn)
            stream(n).wait_recv()
            finish(1, tiles, cols, cols)
    else:
        stream(0).wait_recv()
        for req in range(NUM_REQ):
            put(0, hid, hid_out, req).wait()
            put(1, part, part_out, req).wait()
    incoming.wait_send()
    swap.wait_send()
    for n in range(streamed):
        stream(n).wait_send()


def mlp(hid, own, recv, gain, wg, wu, wd, layer, img_loc, tf=1024, tn=512, nb=2, nd=2):
    rows, width = recv.shape
    ff = wg.shape[2]
    last = layer == NUM_LAYERS - 1
    if last:
        outs = (out(NUM_REQ, img_loc, width), out(NUM_REQ, rows - img_loc, width))
        out_specs = (VMEM_SPEC,) * 2
        extra = [vmem(rows, width), vmem(rows, width)]
    else:
        outs = (out(NUM_REQ * rows, width), out(NUM_REQ * rows, width), out(rows, width), out(rows, tn))
        out_specs = (HBM_SPEC,) * 4
        extra = []
    return pl.pallas_call(
        functools.partial(mlp_kernel, layer, img_loc, tf, tn),
        out_shape=outs,
        in_specs=[HBM_SPEC] * 3 + [VMEM_SPEC] + [ANY_SPEC] * 3,
        out_specs=out_specs,
        scratch_shapes=extra + [
            *[vmem(NUM_REQ * rows, width)] * 4, vmem(rows, width), vmem(rows, ff),
            vmem(nb, width, tf), vmem(nb, width, tf), vmem(nd, ff, tn),
            DMA((5,)), DMA((2 * NUM_REQ,)), DMA((nb,)), DMA((nb,)), DMA((nd,)), DMA((2 + width // tn,)), DMA((2 + width // tn,)),
        ],
        compiler_params=pltpu.CompilerParams(collective_id=NUM_LAYERS + layer, has_side_effects=True, vmem_limit_bytes=63 << 20),
        name=f"mlp{layer}",
    )(hid, own, recv, gain, wg, wu, wd)


def solution(mesh):
    in_specs = (P("dp", "sp", None), P("dp", "sp"), P("dp"), P(), P(), P("tp", None), P(), P(None, None, "tp"), P(), P(), P(None, "tp", None), P(), P(None, None, "tp"), P(None, None, "tp"), P(None, "tp", None))
    out_specs = (P("dp", "sp", None), P("dp", "sp", None), P(None, None, "dp", "sp", None), P(None, None, "dp", "sp", None))

    def device_fn(features, tokens, lengths, proj_w, proj_b, embed, ln_attn, w_query, w_key, w_value, w_out, ln_mlp, w_gate, w_up, w_down):
        img_loc = features.shape[1]
        rows = img_loc + tokens.shape[1]
        half = w_key.shape[2] // 2
        freq = np.power(np.float32(ROPE_THETA), -np.arange(half, dtype=np.float32) * np.float32(1.0 / half)).reshape(1, half)
        sources = (start(tokens, embed),)
        extra = (features, proj_w, proj_b)
        for layer in range(NUM_LAYERS):
            hid, part, recv, *caches = attention(sources, extra, ln_attn, freq, lengths, w_query, w_key, w_value, w_out, layer, rows, img_loc)
            extra = tuple(caches)
            sources = mlp(hid, part, recv, ln_mlp, w_gate, w_up, w_down, layer, img_loc)
        return *sources, *caches

    return jax.shard_map(device_fn, mesh=mesh, in_specs=in_specs, out_specs=out_specs, check_vma=False)
```

time: 312 us -> 294 us (0.942)
  local copies, waits for them, and re-layouts: 20 us -> 6.79 us
  Pallas kernels: 289 us -> 285 us
    unnamed x26 -> x14, local copies, waits for them, and re-layouts: 12.5 us -> 6.79 us
    pallas_call x2, Pallas kernels: 108 us -> 103 us  [attention(): pl.pallas_call(functools.partial(attention_kernel, layer, img_loc), out_s...]
    slice x4 -> x0, local copies, waits for them, and re-layouts: 3.86 us -> none  [the longest x2 1.68 us: device_fn(): return (*sources, cache[:, :, :, :img_loc], cache[:, :, :, img_loc:])]
where the time goes in v4:
time: 294 us; the launch traced here: 293 us
  Pallas kernels  285 us (97%)
  local copies, waits for them, and re-layouts  6.79 us (2%)
    pallas_call x2, Pallas kernels, mlp(): pl.pallas_call(functools.partial(mlp_kernel, layer, img_loc, tf, tn), out...  174 us
    pallas_call x2, Pallas kernels, attention(): pl.pallas_call(functools.partial(attention_kernel, layer, img_loc), out_s...  103 us
    pallas_call x1, Pallas kernels, start(): pl.pallas_call(start_kernel, out_shape=out(num, width), in_specs=[SMEM_SP...  7.95 us
    unnamed x14, local copies, waits for them, and re-layouts  6.79 us

profile of v4, /device:TPU:0, one launch (start us, length us, event | category | flops | bytes accessed | tf_op | source)
XLA Modules:
  0.0 292.9 jit_solution(8461475211767627740)
XLA Ops:
  0.6 0.0 copy-start.1
  0.6 0.7 copy-done.1
  1.3 8.0 %start.1.refs_0_ = bf16[256,2048]{1,0:T(8,128)(2,1)S(1)} custom-call(s32[2,128]{1,0:T(2,128)S(1)} %copy-done.1, s32[2,128]{1,0:T(2,128)S(1)} %copy-done.1, bf16[128000,2048]{1,0:T(8,128)(2,1)} %embed.1), custom_call_target="tpu_custom_call" | custom-call | tf_op jit(solution)/shard_map/start/pallas_call | solution.py:104
  9.3 0.0 copy-start
  9.3 1.0 copy-done
  10.2 55.4 %attention0.1 = (bf16[544,2048]{1,0:T(8,128)(2,1)}, bf16[544,2048]{1,0:T(8,128)(2,1)}, bf16[272,2048]{1,0:T(8,128)(2,1)}, bf16[544,512]{1,0:T(8,128)(2,1)}) custom-call(bf16[256,2048]{1,0:T(8,128)(2,1)} %copy-done, bf16[2,144,1024]{2,1,0:T(8,128)(2,1)} %refs_1_.1, bf16[1024,2048]{1,0:T(8,128)(2,1)} %refs_2_.1, bf16[2048]{0:T(1024)(128)(2,1)} %refs_3_.1, ...), custom_call_target="tpu_custom_call" | custom-call | tf_op jit(solution)/shard_map/attention0/pallas_call | solution.py:326
  65.7 78.6 %mlp0.1 = (bf16[544,2048]{1,0:T(8,128)(2,1)}, bf16[544,2048]{1,0:T(8,128)(2,1)}, bf16[272,2048]{1,0:T(8,128)(2,1)}, bf16[272,512]{1,0:T(8,128)(2,1)}) custom-call(bf16[544,2048]{1,0:T(8,128)(2,1)} %get-tuple-element.19.hid_in, bf16[544,2048]{1,0:T(8,128)(2,1)} %get-tuple-element.20.own_in, bf16[272,2048]{1,0:T(8,128)(2,1)} %get-tuple-element.21.recv0, ...), custom_call_target="tpu_custom_call" | custom-call | tf_op jit(solution)/shard_map/mlp0/pallas_call | solution.py:488
  144.3 48.0 %attention1.1 = (bf16[544,2048]{1,0:T(8,128)(2,1)}, bf16[544,2048]{1,0:T(8,128)(2,1)}, bf16[272,2048]{1,0:T(8,128)(2,1)}, bf16[2,2,2,144,256]{4,3,2,1,0:T(8,128)(2,1)}, bf16[2,2,2,128,256]{4,3,2,1,0:T(8,128)(2,1)}) custom-call(bf16[544,2048]{1,0:T(8,128)(2,1)} %get-tuple-element.22.refs_0_, bf16[544,2048]{1,0:T(8,128)(2,1)} %get-tuple-element.23.refs_1_, ...), custom_call_target="tpu_custom_call" | custom-call | tf_op jit(solution)/shard_map/attention1/pallas_call | solution.py:326
  192.3 95.4 %mlp1.1 = (bf16[2,144,2048]{2,1,0:T(8,128)(2,1)}, bf16[2,128,2048]{2,1,0:T(8,128)(2,1)}) custom-call(bf16[544,2048]{1,0:T(8,128)(2,1)} %get-tuple-element.27.hid_in, bf16[544,2048]{1,0:T(8,128)(2,1)} %get-tuple-element.28.own_in, bf16[272,2048]{1,0:T(8,128)(2,1)} %get-tuple-element.29.recv0, bf16[2,2048]{1,0:T(2,128)(2,1)} %gain.3, ...), custom_call_target="tpu_custom_call" | custom-call | tf_op jit(solution)/shard_map/mlp1/pallas_call | solution.py:488
  287.7 0.0 copy-start.2
  287.7 0.0 copy-start.3
  287.8 0.0 copy-start.4
  287.8 2.6 copy.24
  290.3 0.0 copy-done.2
  290.3 1.0 copy.25
  291.3 0.0 copy-done.3
  291.3 0.8 copy.26
  292.1 0.0 copy-done.4
  292.1 0.8 copy.27
Async XLA Ops:
  0.6 0.7 copy-start.1
  9.3 1.0 copy-start
  287.7 2.6 copy-start.2
  287.7 3.6 %copy-start.3 = (bf16[2,2,2,144,256]{4,3,2,1,0:T(8,128)(2,1)S(1)}, bf16[2,2,2,144,256]{4,3,2,1,0:T(8,128)(2,1)}, u32[]{:S(2)}) copy-start(bf16[2,2,2,144,256]{4,3,2,1,0:T(8,128)(2,1)} %get-tuple-element.40) | copy-start | bytes 1769476
  287.8 4.4 %copy-start.4 = (bf16[2,2,2,128,256]{4,3,2,1,0:T(8,128)(2,1)S(1)}, bf16[2,2,2,128,256]{4,3,2,1,0:T(8,128)(2,1)}, u32[]{:S(2)}) copy-start(bf16[2,2,2,128,256]{4,3,2,1,0:T(8,128)(2,1)} %get-tuple-element.41) | copy-start | bytes 1572868

commit v5 on v4

--- a/solution.py
+++ b/solution.py
@@ -117,10 +117,10 @@
     if first:
         picked, features, proj, bias, *refs = refs
     else:
-        hid_in, mlp_part, mlp_recv, mlp_tile, kv_before, *refs = refs
-    gain, freq, lengths, wq, wk, wv, wo, hid_out, part_out, recv, *refs = refs
+        hid_in, mlp_part, mlp_recv, mlp_tile, wo_twin, kv_before, *refs = refs
+    gain, freq, lengths, wq, wk, wv, wo, hid_out, part_out, *refs = refs
     if first:
-        kv, *refs = refs
+        recv, kv, *refs = refs
     else:
         cache_image, cache_prompt, *refs = refs
     hid, part, x, arrive, kvs, q, o, cos, sin, wq_buf, wk_buf, wv_buf, wo_buf, lsem, osem, tp_send, tp_recv, sp_send, sp_recv, *refs = refs
@@ -143,10 +143,14 @@
         feat_buf, proj_buf = refs
         inputs = [load(4 + req, features.at[req], feat_buf.at[req]) for req in range(NUM_REQ)] + [load(6, proj, proj_buf)]
     else:
-        own, other = refs
+        own, other, o_first, o_twin, wo_twin_buf = refs
         done = mlp_tile.shape[1]
         lower, upper = pl.ds(0, rows), pl.ds(rows, rows)
         inputs = [load(4, hid_in.at[lower], hid.at[lower]), load(5, mlp_part.at[lower], own.at[lower]), load(6, mlp_recv, other), load(7, hid_in.at[upper], hid.at[upper]), load(8, mlp_part.at[upper], own.at[upper]), load(9, mlp_tile, arrive.at[:, pl.ds(0, done)])]
+        share = wo_twin_buf.shape[0] // 4
+        quarters = [ds(k * share, share) for k in (me, near, far)]
+        inputs += [load(10 + k, wo_twin.at[at], wo_twin_buf.at[at]) for k, at in enumerate(quarters)]
+        last_quarter = remote(wo_twin.at[quarters[2]], wo_twin_buf.at[quarters[2]], sp_send.at[3 * NUM_REQ], sp_recv.at[3 * NUM_REQ], {"sp": near})
     for copy in (*inputs[:3], *weights, *inputs[3:]):
         copy.start()
     greet(({"sp": near}, {"sp": far}, twin))
@@ -158,6 +162,8 @@
         arrivals = [remote(mlp_part.at[upper, rest], arrive.at[:, rest], tp_send.at[1], tp_recv.at[1], twin)]
     for arrival in arrivals:
         arrival.start()
+    if not first:
+        last_quarter.start()
     scale = 1.0 + f32(gain[layer:layer + 1, :])
 
     local = lax.broadcasted_iota(jnp.int32, (rows, half), 0)
@@ -221,7 +227,7 @@
     idx = col - slot_of * rows
     text_pos = jnp.where(idx < img_loc, -1, owner * txt_loc + idx - img_loc)
 
-    def attend(req):
+    def attend(req, o):
         for p in range(len(pieces)):
             to_far, _, relay = sends(req, p)
             to_far.wait_recv()
@@ -241,9 +247,13 @@
             p = bf16(e * (1.0 / jnp.sum(e, axis=-1, keepdims=True)))
             o[:, lanes] = bf16(dot32(p, kvs[every, head_dim:]))
         once(3)
-        tile = 2 * head_dim
-        for n in range(width // tile):
-            cols = slice(n * tile, (n + 1) * tile)
+
+    tile = 2 * head_dim
+    out_tiles = [slice(n * tile, (n + 1) * tile) for n in range(width // tile)]
+
+    def project_out(req):
+        here = pl.ds(req * rows, rows)
+        for cols in out_tiles:
             part[here, cols] = bf16(dot32(o[...], wo_buf[:, cols]))
 
     def put(i, src, dst, req):
@@ -251,7 +261,7 @@
         return pltpu.make_async_copy(src.at[here], dst.at[here], osem.at[i])
 
     puts = [put(2 * req + i, src, dst, req) for req in range(NUM_REQ) for i, (src, dst) in enumerate(((hid, hid_out), (part, part_out)))]
-    swap = remote(part.at[pl.ds(0, rows)], recv, tp_send.at[2], tp_recv.at[2], twin)
+    swap = remote(part.at[pl.ds(0, rows)], recv, tp_send.at[2], tp_recv.at[2], twin) if first else remote(o_first, o_twin, tp_send.at[2], tp_recv.at[2], twin)
 
     def keep(at, h):
         hid[at, :] = h
@@ -295,15 +305,29 @@
                 keep(src, add_parts(hid[src, :], own[src, :], incoming[at(0), :]))
 
             each_block(rows, row_block)
-            puts[2 * req].start()
+            if req == 1:
+                puts[2].start()
             project(req, 0)
-        attend(req)
-        puts[2 * req + 1].start()
+        if first or req == 1:
+            attend(req, o)
+            project_out(req)
+            puts[2 * req + 1].start()
+        else:
+            attend(req, o_first)
         if req == 0:
             swap.start()
+    swap.wait_recv()
+    if not first:
+        for copy in inputs[6:]:
+            copy.wait()
+        last_quarter.wait()
+        for cols in out_tiles:
+            total = dot32(o_first[...], wo_buf[:, cols]) + dot32(o_twin[...], wo_twin_buf[:, cols])
+            hid[:rows, cols] = bf16(f32(hid[:rows, cols]) + f32(bf16(total)))
+        puts[0].start()
+        puts = [puts[0], puts[2], puts[3]]
     for copy in puts:
         copy.wait()
-    swap.wait_recv()
     for copy in (*arrivals, swap, *[c for req in range(NUM_REQ) for p in range(len(pieces)) for c in sends(req, p)]):
         copy.wait_send()
 
@@ -316,47 +340,49 @@
     first = layer == 0
     if first:
         specs = [VMEM_SPEC, HBM_SPEC, HBM_SPEC, VMEM_SPEC]
-        outs, out_specs = (out(total, 2 * kw),), (VMEM_SPEC,)
+        outs, out_specs = (out(rows, width), out(total, 2 * kw)), (HBM_SPEC, VMEM_SPEC)
         scratch = [vmem(NUM_REQ, img_loc, extra[0].shape[2]), vmem(*extra[1].shape)]
     else:
-        specs = [HBM_SPEC] * 4 + [VMEM_SPEC]
+        specs = [HBM_SPEC] * 5 + [VMEM_SPEC]
         outs, out_specs = tuple(out(NUM_LAYERS, 2, NUM_REQ, n, kw) for n in (img_loc, txt_loc)), (VMEM_SPEC, VMEM_SPEC)
-        scratch = [vmem(total, width), vmem(rows, width)]
-    copies = NUM_REQ * 3 * (2 if first else 1)
+        scratch = [vmem(total, width), vmem(rows, width), vmem(rows, qw), vmem(rows, qw), vmem(qw, width)]
+    copies = NUM_REQ * 3 * 2
     return pl.pallas_call(
         functools.partial(attention_kernel, layer, img_loc),
-        out_shape=(out(total, width), out(total, width), out(rows, width), *outs),
+        out_shape=(out(total, width), out(total, width), *outs),
         in_specs=specs + [VMEM_SPEC] * 2 + [SMEM_SPEC] + [ANY_SPEC] * 4,
-        out_specs=(HBM_SPEC,) * 3 + out_specs,
+        out_specs=(HBM_SPEC,) * 2 + out_specs,
         scratch_shapes=[
             vmem(total, width), vmem(total, width), vmem(total, width), vmem(NUM_REQ * txt_loc if first else rows, width),
             vmem(NUM_REQ * 4 * rows, 2 * kw), vmem(total, qw), vmem(rows, qw),
             pltpu.VMEM((rows, kw // 2), jnp.float32), pltpu.VMEM((rows, kw // 2), jnp.float32),
             vmem(width, qw), vmem(width, kw), vmem(width, kw), vmem(qw, width),
-            DMA((10,)), DMA((2 * NUM_REQ,)), DMA((3,)), DMA((3,)), DMA((copies,)), DMA((copies,)), *scratch,
+            DMA((13,)), DMA((2 * NUM_REQ,)), DMA((3,)), DMA((3,)), DMA((copies,)), DMA((copies,)), *scratch,
         ],
         compiler_params=pltpu.CompilerParams(collective_id=layer, has_side_effects=True, vmem_limit_bytes=56 << 20),
         name=f"attention{layer}",
     )(*sources, *extra, gain, freq, lengths, wq, wk, wv, wo)
 
 
-def mlp_kernel(layer, img_loc, tf, tn, hid_in, own_in, recv0, gain, wg, wu, wd, *refs):
+def mlp_kernel(layer, img_loc, tf, tn, hid_in, own_in, *refs):
     last = layer == NUM_LAYERS - 1
     if last:
-        image, prompt, recv, tiles, *refs = refs
-    else:
-        hid_out, part_out, recv, tiles, *refs = refs
-    hid, own, part, other, x, act, gbuf, ubuf, dbuf, lsem, osem, gsem, usem, dsem, tp_send, tp_recv = refs
-    rows = recv0.shape[0]
+        gain, wg, wu, wd, image, prompt, recv, tiles, *refs = refs
+    else:
+        recv0, wo, gain, wg, wu, wd, hid_out, part_out, recv, tiles, wo_twin, *refs = refs
+    hid, own, part, other, x, act, gbuf, ubuf, dbuf, lsem, osem, gsem, usem, dsem, tp_send, tp_recv, w_send, w_recv = refs
+    rows = hid_in.shape[0] // NUM_REQ
     lower, upper = pl.ds(0, rows), pl.ds(rows, rows)
-    inputs = [pltpu.make_async_copy(src, dst, lsem.at[i]) for i, (src, dst) in enumerate(((hid_in.at[lower], hid.at[lower]), (own_in.at[lower], own.at[lower]), (recv0, other.at[lower]), (hid_in.at[upper], hid.at[upper]), (own_in.at[upper], own.at[upper])))]
+    inputs = [pltpu.make_async_copy(src, dst, lsem.at[i]) for i, (src, dst) in enumerate(((hid_in.at[lower], hid.at[lower]), (hid_in.at[upper], hid.at[upper]), (own_in.at[upper], own.at[upper]), *(() if last else ((own_in.at[lower], own.at[lower]), (recv0, other.at[lower])))))]
     for copy in inputs:
         copy.start()
     ff, width = wd.shape[1:]
     nf, nn = ff // tf, width // tn
     nb, nd = gbuf.shape[0], dbuf.shape[0]
-    streamed = nn if last else 1
+    pieces = [(n * tn, tn) for n in range(nn)] if last else [(0, tn)]
     twin = {"tp": 1 - lax.axis_index("tp")}
+    me = lax.axis_index("sp")
+    near, far = lax.bitwise_xor(me, 1), lax.bitwise_xor(me, 2)
 
     def load(src, buf, sem, tile, i, slot):
         return pltpu.make_async_copy(src.at[layer, :, ds(i * tile, tile)], buf.at[slot], sem.at[slot])
@@ -367,14 +393,20 @@
     for i in range(nb):
         gload(i, i).start()
         uload(i, i).start()
-    greet((twin,))
+    greet((twin,) if last else (twin, {"sp": near}, {"sp": far}))
     incoming = remote(own_in.at[upper], other.at[upper], tp_send.at[0], tp_recv.at[0], twin)
     incoming.start()
     swap = remote(part.at[lower], recv, tp_send.at[1], tp_recv.at[1], twin)
 
     def stream(n):
-        cols = ds(n * tn, tn)
+        cols = pl.ds(*pieces[n])
         return remote(part.at[upper, cols], tiles.at[:, cols], tp_send.at[2 + n], tp_recv.at[2 + n], twin)
+
+    if not last:
+        share = wo.shape[1] // 4
+        mine = ds(me * share, share)
+        ahead = wo.at[layer + 1, mine]
+        hops = [remote(src, wo_twin.at[mine], w_send.at[i], w_recv.at[i], peer) for i, (src, peer) in enumerate(((ahead, twin), (wo_twin.at[mine], {"sp": far}), (wo_twin.at[mine], {"sp": near})))]
 
     scale = 1.0 + f32(gain[layer:layer + 1, :])
     for copy in inputs:
@@ -396,21 +428,40 @@
             hid[src, :] = h
             x[at(0), :] = normed(h, scale)
 
-        each_block(rows, row_block)
-        if not last:
+        def ready_block(at):
+            x[at(0), :] = normed(hid[at(0), :], scale)
+
+        if last:
+            pl.when(req == 0)(lambda: each_block(rows, ready_block))
+            pl.when(req == 1)(lambda: each_block(rows, row_block))
+        else:
+            each_block(rows, row_block)
             put(0, hid, hid_out, req).start()
 
         @pl.loop(0, nf)
         def _(i):
             slot = lax.rem(i, nb)
             gload(i, slot).wait()
+            if not last:
+                pl.when((req == 0) & (i == nf // 2))(hops[0].start)
+
+                @pl.when((req == 1) & (i == nf // 2))
+                def _():
+                    hops[0].wait_recv()
+                    hops[1].start()
+                    hops[2].start()
+
             gate = dot32(x[...], gbuf[slot])
-            uload(i, slot).wait()
-            act[:, ds(i * tf, tf)] = bf16(gelu_tanh(gate) * dot32(x[...], ubuf[slot]))
 
             @pl.when(i + nb < nf)
             def _():
                 gload(i + nb, slot).start()
+
+            uload(i, slot).wait()
+            act[:, ds(i * tf, tf)] = bf16(gelu_tanh(gate) * dot32(x[...], ubuf[slot]))
+
+            @pl.when(i + nb < nf)
+            def _():
                 uload(i + nb, slot).start()
 
             @pl.when((i + nb >= nf) & (i + nb < nf + nd))
@@ -432,9 +483,8 @@
                 gload(i + nd - nn, i + nd - nn).start()
                 uload(i + nd - nn, i + nd - nn).start()
 
-            @pl.when((req == 1) & (i < streamed))
-            def _():
-                stream(i).start()
+            for n, (col, _) in enumerate(pieces):
+                pl.when((req == 1) & (i == col // tn))(stream(n).start)
 
         if not last:
             put(1, part, part_out, req).start()
@@ -463,18 +513,23 @@
             stream(n).wait_recv()
             finish(1, tiles, cols, cols)
     else:
-        stream(0).wait_recv()
+        for n in range(len(pieces)):
+            stream(n).wait_recv()
+        hops[1].wait_recv()
+        hops[2].wait_recv()
+        for hop in hops:
+            hop.wait_send()
         for req in range(NUM_REQ):
             put(0, hid, hid_out, req).wait()
             put(1, part, part_out, req).wait()
     incoming.wait_send()
     swap.wait_send()
-    for n in range(streamed):
+    for n in range(len(pieces)):
         stream(n).wait_send()
 
 
-def mlp(hid, own, recv, gain, wg, wu, wd, layer, img_loc, tf=1024, tn=512, nb=2, nd=2):
-    rows, width = recv.shape
+def mlp(sources, gain, wg, wu, wd, layer, img_loc, tf=1024, tn=512, nb=2, nd=2):
+    rows, width = sources[0].shape[0] // NUM_REQ, sources[0].shape[1]
     ff = wg.shape[2]
     last = layer == NUM_LAYERS - 1
     if last:
@@ -482,22 +537,22 @@
         out_specs = (VMEM_SPEC,) * 2
         extra = [vmem(rows, width), vmem(rows, width)]
     else:
-        outs = (out(NUM_REQ * rows, width), out(NUM_REQ * rows, width), out(rows, width), out(rows, tn))
-        out_specs = (HBM_SPEC,) * 4
+        outs = (out(NUM_REQ * rows, width), out(NUM_REQ * rows, width), out(rows, width), out(rows, tn), out(*sources[3].shape[1:]))
+        out_specs = (HBM_SPEC,) * 5
         extra = []
     return pl.pallas_call(
         functools.partial(mlp_kernel, layer, img_loc, tf, tn),
         out_shape=outs,
-        in_specs=[HBM_SPEC] * 3 + [VMEM_SPEC] + [ANY_SPEC] * 3,
+        in_specs=[HBM_SPEC] * len(sources) + [VMEM_SPEC] + [ANY_SPEC] * 3,
         out_specs=out_specs,
         scratch_shapes=extra + [
             *[vmem(NUM_REQ * rows, width)] * 4, vmem(rows, width), vmem(rows, ff),
             vmem(nb, width, tf), vmem(nb, width, tf), vmem(nd, ff, tn),
-            DMA((5,)), DMA((2 * NUM_REQ,)), DMA((nb,)), DMA((nb,)), DMA((nd,)), DMA((2 + width // tn,)), DMA((2 + width // tn,)),
+            DMA((5,)), DMA((2 * NUM_REQ,)), DMA((nb,)), DMA((nb,)), DMA((nd,)), DMA((2 + width // tn,)), DMA((2 + width // tn,)), DMA((3,)), DMA((3,)),
         ],
         compiler_params=pltpu.CompilerParams(collective_id=NUM_LAYERS + layer, has_side_effects=True, vmem_limit_bytes=63 << 20),
         name=f"mlp{layer}",
-    )(hid, own, recv, gain, wg, wu, wd)
+    )(*sources, gain, wg, wu, wd)
 
 
 def solution(mesh):
@@ -512,9 +567,12 @@
         sources = (start(tokens, embed),)
         extra = (features, proj_w, proj_b)
         for layer in range(NUM_LAYERS):
-            hid, part, recv, *caches = attention(sources, extra, ln_attn, freq, lengths, w_query, w_key, w_value, w_out, layer, rows, img_loc)
-            extra = tuple(caches)
-            sources = mlp(hid, part, recv, ln_mlp, w_gate, w_up, w_down, layer, img_loc)
+            hid, part, *caches = attention(sources, extra, ln_attn, freq, lengths, w_query, w_key, w_value, w_out, layer, rows, img_loc)
+            sources = (hid, part)
+            if layer == 0:
+                recv, *extra = caches
+                sources = (hid, part, recv, w_out)
+            sources = mlp(sources, ln_mlp, w_gate, w_up, w_down, layer, img_loc)
         return *sources, *caches
 
     return jax.shard_map(device_fn, mesh=mesh, in_specs=in_specs, out_specs=out_specs, check_vma=False)

time: 294 us -> 287 us (0.976)
  Pallas kernels: 285 us -> 279 us
    pallas_call x2, Pallas kernels: 103 us -> 96.2 us  [attention(): pl.pallas_call(functools.partial(attention_kernel, layer, img_loc), out_s...]
where the time goes in v5:
time: 287 us; the launch traced here: 286 us
  Pallas kernels  279 us (97%)
  local copies, waits for them, and re-layouts  6.79 us (2%)
    pallas_call x2, Pallas kernels, mlp(): pl.pallas_call(functools.partial(mlp_kernel, layer, img_loc, tf, tn), out...  175 us
    pallas_call x2, Pallas kernels, attention(): pl.pallas_call(functools.partial(attention_kernel, layer, img_loc), out_s...  96.2 us
    pallas_call x1, Pallas kernels, start(): pl.pallas_call(start_kernel, out_shape=out(num, width), in_specs=[SMEM_SP...  7.71 us
    unnamed x14, local copies, waits for them, and re-layouts  6.79 us

profile of v5, /device:TPU:0, one launch (start us, length us, event | category | flops | bytes accessed | tf_op | source)
XLA Modules:
  0.0 286.3 jit_solution(10803147202136252169)
XLA Ops:
  0.6 0.0 copy-start.1
  0.6 0.7 copy-done.1
  1.3 7.7 %start.1.refs_0_ = bf16[256,2048]{1,0:T(8,128)(2,1)S(1)} custom-call(s32[2,128]{1,0:T(2,128)S(1)} %copy-done.1, s32[2,128]{1,0:T(2,128)S(1)} %copy-done.1, bf16[128000,2048]{1,0:T(8,128)(2,1)} %embed.1), custom_call_target="tpu_custom_call" | custom-call | tf_op jit(solution)/shard_map/start/pallas_call | solution.py:104
  9.0 0.0 copy-start
  9.0 1.0 copy-done
  10.0 55.6 %attention0.1 = (bf16[544,2048]{1,0:T(8,128)(2,1)}, bf16[544,2048]{1,0:T(8,128)(2,1)}, bf16[272,2048]{1,0:T(8,128)(2,1)}, bf16[544,512]{1,0:T(8,128)(2,1)}) custom-call(bf16[256,2048]{1,0:T(8,128)(2,1)} %copy-done, bf16[2,144,1024]{2,1,0:T(8,128)(2,1)} %refs_1_.3, bf16[1024,2048]{1,0:T(8,128)(2,1)} %refs_2_.3, bf16[2048]{0:T(1024)(128)(2,1)} %refs_3_.3, ...), custom_call_target="tpu_custom_call" | custom-call | tf_op jit(solution)/shard_map/attention0/pallas_call | solution.py:350
  65.6 80.3 %mlp0.1 = (bf16[544,2048]{1,0:T(8,128)(2,1)}, bf16[544,2048]{1,0:T(8,128)(2,1)}, bf16[272,2048]{1,0:T(8,128)(2,1)}, bf16[272,512]{1,0:T(8,128)(2,1)}, bf16[1024,2048]{1,0:T(8,128)(2,1)}) custom-call(bf16[544,2048]{1,0:T(8,128)(2,1)} %get-tuple-element.19.hid_in, bf16[544,2048]{1,0:T(8,128)(2,1)} %get-tuple-element.20.own_in, ...), custom_call_target="tpu_custom_call" | custom-call | tf_op jit(solution)/shard_map/mlp0/pallas_call | solution.py:543
  145.9 40.6 %attention1.1 = (bf16[544,2048]{1,0:T(8,128)(2,1)}, bf16[544,2048]{1,0:T(8,128)(2,1)}, bf16[2,2,2,144,256]{4,3,2,1,0:T(8,128)(2,1)}, bf16[2,2,2,128,256]{4,3,2,1,0:T(8,128)(2,1)}) custom-call(bf16[544,2048]{1,0:T(8,128)(2,1)} %get-tuple-element.22.refs_0_, bf16[544,2048]{1,0:T(8,128)(2,1)} %get-tuple-element.23.refs_1_, ...), custom_call_target="tpu_custom_call" | custom-call | tf_op jit(solution)/shard_map/attention1/pallas_call | solution.py:350
  186.5 94.5 %mlp1.1 = (bf16[2,144,2048]{2,1,0:T(8,128)(2,1)}, bf16[2,128,2048]{2,1,0:T(8,128)(2,1)}) custom-call(bf16[544,2048]{1,0:T(8,128)(2,1)} %get-tuple-element.28.hid_in, bf16[544,2048]{1,0:T(8,128)(2,1)} %get-tuple-element.29.own_in, bf16[2,2048]{1,0:T(2,128)(2,1)} %refs_0_.1, bf16[2,2048,8192]{2,1,0:T(8,128)(2,1)} %refs_1_.5, bf16[2,2048,8192]{2,1,0:T(8,128)(2,1)} %refs_2_.5, ...), custom_call_target="tpu_custom_call" | custom-call | tf_op jit(solution)/shard_map/mlp1/pallas_call | solution.py:543
  281.1 0.0 copy-start.2
  281.1 0.0 copy-start.3
  281.1 0.0 copy-start.4
  281.1 2.6 copy.24
  283.7 0.0 copy-done.2
  283.7 1.0 copy.25
  284.6 0.0 copy-done.3
  284.6 0.8 copy.26
  285.5 0.0 copy-done.4
  285.5 0.8 copy.27
Async XLA Ops:
  0.6 0.7 copy-start.1
  9.0 1.0 copy-start
  281.1 2.6 copy-start.2
  281.1 3.6 %copy-start.3 = (bf16[2,2,2,144,256]{4,3,2,1,0:T(8,128)(2,1)S(1)}, bf16[2,2,2,144,256]{4,3,2,1,0:T(8,128)(2,1)}, u32[]{:S(2)}) copy-start(bf16[2,2,2,144,256]{4,3,2,1,0:T(8,128)(2,1)} %get-tuple-element.40) | copy-start | bytes 1769476
  281.1 4.4 %copy-start.4 = (bf16[2,2,2,128,256]{4,3,2,1,0:T(8,128)(2,1)S(1)}, bf16[2,2,2,128,256]{4,3,2,1,0:T(8,128)(2,1)}, u32[]{:S(2)}) copy-start(bf16[2,2,2,128,256]{4,3,2,1,0:T(8,128)(2,1)} %get-tuple-element.41) | copy-start | bytes 1572868
